TPU v7x, 256 devices: a whole 4x4x8 slice. The times are simulated.
256 devices in a mesh: row: 16 (over z, y_hi), ma: 16 (over y_lo, x, core).
Axes of the slice: x: 4, y: 4 (y_hi: 2, y_lo: 2; y = y_hi * 2 + y_lo), z: 8, core: 2. Of those that a mesh axis runs over, the one named last changes fastest.
Arguments:
- thermal_state: float32 [128, 768, 2048], P('row', None, 'ma'), may hold values from -6 to 6
- sphere_node_annulus: int32 [128, 768], P('row'), may hold values from 0 to 1022, as said below
- sphere_node_offset: float32 [128, 768], P('row'), may hold values from 0 to 1
- integration_share: float32 [128, 768], P('row'), may hold values from 0.02 to 0.2
- annulus_holder_row: int32 [1024], replicated, may hold values from 0 to 15, never falling along the last dimension, each value on 1 to 128 neighbouring positions
- rotating_flow_potential: float32 [2048, 2048], P('row', 'ma'), may hold values from -6 to 6
Outputs:
- thermal_state_later: float32 [128, 768, 2048], P('row', None, 'ma')
- flow_potential_later: float32 [2048, 2048], P('row', 'ma')
Inputs may be any that keep to these rules, and one draw needn't show every extreme that they name: `sphere_node_annulus`: lower cell of each point; the next cell exists. `annulus_holder_row`: never falling along cells; each owner holds 1 to 128 cells and some owner exactly 128.
All inputs are finite; a program needn't handle non-finite values.
Results may differ from a plain program's by a relative error of at most 0.0003.
Values sent between devices are 32-bit elements; how exact they have to be, the bound alone decides.
A program may use at most 64 MiB of HBM per device.

v0:
```python
import math

import jax
import jax.numpy as jnp
from jax import lax
from jax.sharding import PartitionSpec as P

stream_step = 0.5
thermal_advance = 0.25


def extended(x, sides, width, wrap):
    for axis, dim in sides:
        size, length = (lax.axis_size(axis), x.shape[dim])
        up = [(i, (i + 1) % size) for i in range(size if wrap else size - 1)]
        down = [(j, i) for i, j in up]
        last = lax.slice_in_dim(x, length - width, length, axis=dim)
        leading = lax.slice_in_dim(x, 0, width, axis=dim)
        before = lax.ppermute(last, axis, up)
        after = lax.ppermute(leading, axis, down)
        x = jnp.concatenate([before, x, after], axis=dim)
    return x


def in_blocks(x, dim, length):
    before, after = (x.shape[:dim], x.shape[dim + 1 :])
    return jnp.moveaxis(x.reshape(*before, length, -1, *after), dim, 0)


def sum_at_owner(x, axis, dim):
    parts = in_blocks(x, dim, lax.axis_size(axis))
    arrived = lax.all_to_all(parts, axis, split_axis=0, concat_axis=0, tiled=True)
    return arrived.sum(axis=0)


def laid_out(parts, dim):
    parts = jnp.moveaxis(parts, 0, dim)
    lengths = parts.shape
    return parts.reshape(*lengths[:dim], lengths[dim] * lengths[dim + 1], *lengths[dim + 2 :])


def copy_for_each(x, axis):
    length = lax.axis_size(axis)
    return lax.all_to_all(jnp.broadcast_to(x[None], (length, *x.shape)), axis, 0, 0, tiled=True)


def collect(x, axis, dim):
    return laid_out(copy_for_each(x, axis), dim)


def phi_diff(field):
    return (field[:, 2:] - field[:, :-2]) * 0.5


def qg_step(zint, stream, geo_slots):
    geo_column = geo_slots[:, None]
    extended_field = extended(jnp.stack([zint, stream]), (("ma", 2),), 2, True)
    forcing = -geo_column * phi_diff(extended_field[0])
    stream_wide = extended_field[1][:, 1:-1] + stream_step * forcing
    velocity = geo_column * phi_diff(stream_wide)
    return (stream_wide[:, 1:-1], velocity)


def per_device(
    thermal_state,
    sphere_node_annulus,
    sphere_node_offset,
    integration_share,
    annulus_holder_row,
    rotating_flow_potential,
):
    sphere_level_list, meridian_total, longitude_total = thermal_state.shape
    slot_most = rotating_flow_potential.shape[0]
    cell_count = annulus_holder_row.shape[0]
    cells = jnp.arange(cell_count, dtype=jnp.int32)
    before = jnp.sum(
        (annulus_holder_row[None, :] < annulus_holder_row[:, None]).astype(jnp.int32), axis=1
    )
    slot_of_cell = annulus_holder_row * slot_most + cells - before
    geo_cell = 1.0 / (0.25 + (cells.astype(jnp.float32) + 0.5) / cell_count)
    lower_cell = sphere_node_annulus.reshape(-1)
    slot_low = slot_of_cell[lower_cell]
    slot_high = slot_of_cell[lower_cell + 1]
    fraction = sphere_node_offset.reshape(-1)
    quadrature = integration_share.reshape(-1)
    below_share = quadrature * (1.0 - fraction)
    above_share = quadrature * fraction
    heat_vector_linear = thermal_state.reshape(-1, longitude_total)
    own_index = lax.axis_index("row")
    own_start = own_index * slot_most
    slot_rows = jnp.arange(slot_most * lax.axis_size("row"), dtype=jnp.int32)
    banded = jnp.where(slot_rows[:, None] == slot_low[None, :], below_share[None, :], 0.0)
    banded = banded + jnp.where(slot_rows[:, None] == slot_high[None, :], above_share[None, :], 0.0)
    zint = sum_at_owner(
        jnp.dot(
            banded,
            heat_vector_linear,
            precision=lax.Precision.HIGHEST,
            preferred_element_type=jnp.float32,
        ),
        "row",
        0,
    )
    slot_rows = own_start + jnp.arange(slot_most, dtype=jnp.int32)
    hits = slot_of_cell[None, :] == slot_rows[:, None]
    flow_potential_later, velocity = qg_step(
        zint, rotating_flow_potential, jnp.sum(jnp.where(hits, geo_cell[None, :], 0.0), axis=1)
    )
    piece = collect(velocity, "row", 0)
    slot_cols = jnp.arange(piece.shape[0], dtype=jnp.int32)
    interp = jnp.where(slot_low[:, None] == slot_cols[None, :], (1.0 - fraction)[:, None], 0.0)
    interp = interp + jnp.where(slot_high[:, None] == slot_cols[None, :], fraction[:, None], 0.0)
    shifted_heat = jnp.dot(
        interp, piece, precision=lax.Precision.HIGHEST, preferred_element_type=jnp.float32
    )
    sphere_node_drift = shifted_heat.reshape(sphere_level_list, meridian_total, longitude_total)
    annulus_edges = extended(thermal_state, (("row", 0),), 1, False)
    distance_from_centre = (annulus_edges[2:] - annulus_edges[:-2]) * 0.5
    wrapped_heat_grid = jnp.pad(thermal_state, ((0, 0), (1, 1), (0, 0)))
    theta_from_north = (wrapped_heat_grid[:, 2:] - wrapped_heat_grid[:, :-2]) * 0.5
    angle = math.pi * (jnp.arange(meridian_total, dtype=jnp.float32) + 0.5) / meridian_total
    sin_theta_term = jnp.sin(angle)[None, :, None]
    cos_theta_term = jnp.cos(angle)[None, :, None]
    thermal_state_later = thermal_state - thermal_advance * sphere_node_drift * (
        sin_theta_term * distance_from_centre + cos_theta_term * theta_from_north
    )
    return (thermal_state_later, flow_potential_later)


def solution(mesh):
    return jax.shard_map(
        per_device,
        mesh=mesh,
        in_specs=(
            P("row", None, "ma"),
            P("row", None),
            P("row", None),
            P("row", None),
            P(),
            P("row", "ma"),
        ),
        out_specs=(P("row", None, "ma"), P("row", "ma")),
        check_vma=False,
    )
```

profile of v0, /device:TPU:2, one launch (start us, length us, event | category | flops | bytes accessed | tf_op | source)
XLA Modules:
  0.0 240.2 jit_solution(4635380613796594416)
XLA Ops:
  0.6 1.3 convert_reduce_fusion
  2.0 0.7 add_subtract_fusion
  2.7 0.8 copy.8
  3.4 0.7 reshape.234
  4.2 0.7 reshape.235
  4.9 0.1 compare_select_fusion.1
  5.0 24.8 %gather_fusion = s32[6144]{0:T(1024)S(1)} fusion(s32[1024]{0:T(1024)S(1)} %add_subtract_fusion, s32[6144]{0:T(1024)S(1)} %broadcast_clamp_fusion.1), kind=kCustom, calls=%fused_computation | custom fusion | bytes 73728 | tf_op jit(solution)/shard_map/gather | solution.py:82
  29.8 0.0 copy-start.1
  29.8 24.8 %gather_fusion.1 = s32[6144]{0:T(1024)S(1)} fusion(s32[1024]{0:T(1024)S(1)} %add_subtract_fusion, s32[6144]{0:T(1024)S(1)} %broadcast_clamp_fusion), kind=kCustom, calls=%fused_computation.1 | custom fusion | bytes 73728 | tf_op jit(solution)/shard_map/gather | solution.py:83
  54.6 0.0 copy-done.1
  54.6 45.8 %fusion.2 = f32[16,128,128]{2,1,0:T(8,128)} fusion(f32[6144,128,1]{1,0,2:T(8,128)S(1)} %bitcast.33, f32[6144]{0:T(1024)S(1)} %get-tuple-element.11, s32[6144]{0:T(1024)S(1)} %gather_fusion.1, f32[6144]{0:T(1024)S(1)} %get-tuple-element.10, s32[6144]{0:T(1024)S(1)} %gather_fusion, s32[16,128]{1,0:T(8,128)S(1)} %multiply_add_fusion), kind=kOutput, calls=%fused_computation.4 | convolution fusion | flops 19390267392 | bytes 4300800 | tf_op jit(solution)/shard_map/dot_general | solution.py:95
  100.4 0.0 copy-start
  100.4 11.3 %all-to-all-start = ((f32[16,128,128]{2,1,0:T(8,128)}), f32[16,128,128]{2,1,0:T(8,128)S(1)}, u32[]{:S(2)}, u32[]{:S(2)}) async-start(f32[16,128,128]{2,1,0:T(8,128)} %fusion.2), calls=%async_computation | async-start | bytes 2097152 | tf_op jit(solution)/shard_map/all_to_all | solution.py:32
  111.7 0.2 select_reduce_fusion
  111.9 30.0 %all-to-all-done = f32[16,128,128]{2,1,0:T(8,128)S(1)} async-done(((f32[16,128,128]{2,1,0:T(8,128)}), f32[16,128,128]{2,1,0:T(8,128)S(1)}, u32[]{:S(2)}, u32[]{:S(2)}) %all-to-all-start) | async-done | bytes 1048608 | tf_op jit(solution)/shard_map/all_to_all | solution.py:32
  141.9 0.1 reduce_sum.28
  142.0 0.0 copy-done
  142.0 0.1 slice_maximum_fusion
  142.1 0.1 collective-permute-start
  142.2 1.7 collective-permute-start.1
  143.9 2.6 %collective-permute-done = f32[2,128,2]{2,1,0:T(8,128)S(1)} collective-permute-done((f32[2,128,2]{2,1,0:T(8,128)S(1)}, f32[2,128,2]{2,1,0:T(8,128)S(1)}, u32[]{:S(2)}, u32[]{:S(2)}) %collective-permute-start) | collective-permute-done | bytes 2080 | tf_op jit(solution)/shard_map/ppermute | solution.py:19
  146.6 0.0 collective-permute-done.1
  146.6 0.2 pad_maximum_fusion.2
  146.8 0.0 copy-start.2
  146.8 0.1 fusion.31
  146.9 0.7 fusion.36
  147.7 1.1 broadcast_in_dim.83
  148.8 3.7 %all-to-all-start.1 = ((f32[16,128,128]{2,1,0:T(8,128)}), f32[16,128,128]{2,1,0:T(8,128)S(1)}, u32[]{:S(2)}, u32[]{:S(2)}) async-start(f32[16,128,128]{2,1,0:T(8,128)} %broadcast_in_dim.83), calls=%async_computation.1 | async-start | bytes 2097152 | tf_op jit(solution)/shard_map/all_to_all | solution.py:44
  152.4 1.2 fusion.35
  153.6 1.3 collective-permute-start.2
  154.9 6.1 %collective-permute-start.3 = (f32[1,768,128]{2,1,0:T(8,128)S(1)}, f32[1,768,128]{2,1,0:T(8,128)S(1)}, u32[]{:S(2)}, u32[]{:S(2)}) collective-permute-start(f32[1,768,128]{2,1,0:T(8,128)S(1)} %get-tuple-element.3), channel_id=1, source_target_pairs={{0,16},{16,32},{32,48},{48,64},{64,80},{80,96},{96,112},{112,128},... | collective-permute-start | bytes 1179656 | tf_op jit(solution)/shard_map/ppermute | solution.py:19
  161.1 0.0 copy-done.2
  161.1 8.2 %collective-permute-done.2 = f32[1,768,128]{2,1,0:T(8,128)S(1)} collective-permute-done((f32[1,768,128]{2,1,0:T(8,128)S(1)}, f32[1,768,128]{2,1,0:T(8,128)S(1)}, u32[]{:S(2)}, u32[]{:S(2)}) %collective-permute-start.2) | collective-permute-done | bytes 393248 | tf_op jit(solution)/shard_map/ppermute | solution.py:20
  169.3 18.8 %collective-permute-done.3 = f32[1,768,128]{2,1,0:T(8,128)S(1)} collective-permute-done((f32[1,768,128]{2,1,0:T(8,128)S(1)}, f32[1,768,128]{2,1,0:T(8,128)S(1)}, u32[]{:S(2)}, u32[]{:S(2)}) %collective-permute-start.3) | collective-permute-done | bytes 393248 | tf_op jit(solution)/shard_map/ppermute | solution.py:19
  188.1 0.0 all-to-all-done.1
  188.1 52.1 %fusion.26 = f32[8,768,128]{2,1,0:T(8,128)} fusion(f32[8,768,128]{2,1,0:T(8,128)} %param.6, f32[1,768,128]{2,1,0:T(8,128)S(1)} %collective-permute-done.3, f32[1,768,128]{2,1,0:T(8,128)S(1)} %collective-permute-done.2, f32[2048,128,1]{1,0,2:T(8,128)S(1)} %bitcast.28, f32[8,768]{1,0:T(8,128)S(1)} %copy-done.2, s32[8,768]{1,0:T(8,128)S(1)} %eq.121, ...), kind=kOutput, calls=%fused_computation.32 | convolution fusion | flops 19398131712 | bytes 8230912 | tf_op jit(solution)/shard_map/dot_general | solution.py:113
  (12 shorter events, 0.1 us)
Async XLA Ops:
  29.8 24.8 %copy-start.1 = (f32[8,768,128]{2,1,0:T(8,128)S(1)}, f32[8,768,128]{2,1,0:T(8,128)}, u32[]{:S(2)}) copy-start(f32[8,768,128]{2,1,0:T(8,128)} %param.6) | copy-start | bytes 9437188
  100.4 41.6 %copy-start = (f32[128,128]{1,0:T(8,128)S(1)}, f32[128,128]{1,0:T(8,128)}, u32[]{:S(2)}) copy-start(f32[128,128]{1,0:T(8,128)} %param.11) | copy-start | bytes 196612
  100.4 41.6 %all-to-all-start = ((f32[16,128,128]{2,1,0:T(8,128)}), f32[16,128,128]{2,1,0:T(8,128)S(1)}, u32[]{:S(2)}, u32[]{:S(2)}) async-start(f32[16,128,128]{2,1,0:T(8,128)} %fusion.2), calls=%async_computation | async-start | bytes 2097152 | tf_op jit(solution)/shard_map/all_to_all | solution.py:32
  142.1 4.5 %collective-permute-start = (f32[2,128,2]{2,1,0:T(8,128)S(1)}, f32[2,128,2]{2,1,0:T(8,128)S(1)}, u32[]{:S(2)}, u32[]{:S(2)}) collective-permute-start(f32[2,128,2]{2,1,0:T(8,128)S(1)} %get-tuple-element.8), channel_id=1, source_target_pairs={{0,1},{1,2},{2,3},{3,4},{4,5},{5,6},{6,7},{7,8},{8,9},{9,10},{10,1... | collective-permute-start | bytes 6152 | tf_op jit(solution)/shard_map/ppermute | solution.py:19
  142.2 4.4 %collective-permute-start.1 = (f32[2,128,2]{2,1,0:T(8,128)S(1)}, f32[2,128,2]{2,1,0:T(8,128)S(1)}, u32[]{:S(2)}, u32[]{:S(2)}) collective-permute-start(f32[2,128,2]{2,1,0:T(8,128)S(1)} %get-tuple-element.9), channel_id=1, source_target_pairs={{1,0},{2,1},{3,2},{4,3},{5,4},{6,5},{7,6},{8,7},{9,8},{10,9},{11,1... | collective-permute-start | bytes 6152 | tf_op jit(solution)/shard_map/ppermute | solution.py:20
  146.8 14.3 %copy-start.2 = (f32[8,768]{1,0:T(8,128)S(1)}, f32[8,768]{1,0:T(8,128)}, u32[]{:S(2)}) copy-start(f32[8,768]{1,0:T(8,128)} %param.8) | copy-start | bytes 73732
  148.8 39.4 %all-to-all-start.1 = ((f32[16,128,128]{2,1,0:T(8,128)}), f32[16,128,128]{2,1,0:T(8,128)S(1)}, u32[]{:S(2)}, u32[]{:S(2)}) async-start(f32[16,128,128]{2,1,0:T(8,128)} %broadcast_in_dim.83), calls=%async_computation.1 | async-start | bytes 2097152 | tf_op jit(solution)/shard_map/all_to_all | solution.py:44
  153.6 15.7 %collective-permute-start.2 = (f32[1,768,128]{2,1,0:T(8,128)S(1)}, f32[1,768,128]{2,1,0:T(8,128)S(1)}, u32[]{:S(2)}, u32[]{:S(2)}) collective-permute-start(f32[1,768,128]{2,1,0:T(8,128)S(1)} %get-tuple-element.2), channel_id=1, source_target_pairs={{16,0},{32,16},{48,32},{64,48},{80,64},{96,80},{112,96},{128,112},... | collective-permute-start | bytes 1179656 | tf_op jit(solution)/shard_map/ppermute | solution.py:20
  154.9 33.2 %collective-permute-start.3 = (f32[1,768,128]{2,1,0:T(8,128)S(1)}, f32[1,768,128]{2,1,0:T(8,128)S(1)}, u32[]{:S(2)}, u32[]{:S(2)}) collective-permute-start(f32[1,768,128]{2,1,0:T(8,128)S(1)} %get-tuple-element.3), channel_id=1, source_target_pairs={{0,16},{16,32},{32,48},{48,64},{64,80},{80,96},{96,112},{112,128},... | collective-permute-start | bytes 1179656 | tf_op jit(solution)/shard_map/ppermute | solution.py:19
where the time goes:
time: 243 us; the launch traced here: 240 us
  matrix products  97.9 us (40%)
  waiting for transfers between devices  59.7 us (25%)
  local copies, waits for them, and re-layouts  54.1 us (22%)
  starting transfers between devices  24.2 us (10%)
  other arithmetic  3.57 us (1%)
    dot_general x1, matrix products, per_device(): jnp.dot(interp, piece, precision=lax.Precision.HIGHEST, preferred_element...  52.1 us
    dot_general x1, matrix products, per_device(): jnp.dot(banded, heat_vector_linear, precision=lax.Precision.HIGHEST, pref...  45.8 us
    all_to_all x1, waiting for transfers between devices, sum_at_owner(): lax.all_to_all(parts, axis, split_axis=0, concat_axis=0, tiled=True)  30 us
    gather x1, local copies, waits for them, and re-layouts, per_device(): slot_low = slot_of_cell[lower_cell]  24.8 us
    gather x1, local copies, waits for them, and re-layouts, per_device(): slot_high = slot_of_cell[lower_cell + 1]  24.8 us
    ppermute x2, waiting for transfers between devices, extended(): before = lax.ppermute(last, axis, up)  21.5 us
    all_to_all x1, starting transfers between devices, sum_at_owner(): lax.all_to_all(parts, axis, split_axis=0, concat_axis=0, tiled=True)  11.3 us
    ppermute x2, waiting for transfers between devices, extended(): after = lax.ppermute(leading, axis, down)  8.23 us
  transfers between devices with their start and end apart: 6, of which 4 were waited for; matrix products, arithmetic and copies ran while one was open for 1% of the time, Pallas kernels for 0%

commit v1 on v0

v1 whole, which is shorter than its diff:
```python
import functools
import math

import jax
import jax.numpy as jnp
import numpy as np
from jax import lax
from jax.experimental import pallas as pl
from jax.experimental.pallas import tpu as pltpu
from jax.sharding import PartitionSpec as P

MESH = pl.DeviceIdType.MESH
F32 = jnp.float32
BF16 = jnp.bfloat16
N_ROW = 16
N_MA = 16
NT = (((1,), (1,)), ((), ()))


def two_parts(x):
    hi = x.astype(BF16)
    return hi, (x - hi.astype(F32)).astype(BF16)


def one_hot(rows, first, index):
    at = lax.broadcasted_iota(jnp.int32, (rows, index.shape[1]), 0)
    return jnp.where(at == index - first, 1.0, 0.0).astype(BF16)


def geo_row(cells):
    c = lax.broadcasted_iota(jnp.int32, (1, cells), 1).astype(F32)
    return 1.0 / (0.25 + (c + 0.5) / cells)


def own_slots(holder, me, slots):
    cells = holder.shape[1]
    start = jnp.sum((holder < me).astype(F32), axis=1, keepdims=True).astype(jnp.int32)
    c = lax.broadcasted_iota(jnp.int32, (1, cells), 1)
    return one_hot(slots, 0, jnp.where(holder == me, c - start, -1))


def integrate_kernel(t_hbm, low_ref, off_ref, share_ref, holder_ref, stream_ref, sp_ref, edge_ref, tv, twt, lower_sum, upper_sum, sems):
    levels, nodes, width = tv.shape
    cells = holder_ref.shape[1]
    tile = 256
    copies = [pltpu.make_async_copy(t_hbm.at[r], tv.at[r], sems.at[r]) for r in range(levels)]
    for copy in copies:
        copy.start()
    me = lax.axis_index("row")
    geo = geo_row(cells)
    spots = own_slots(holder_ref[...], me, stream_ref.shape[0])
    stream = jnp.concatenate(two_parts(stream_ref[...].T), axis=0)
    placed = jnp.dot(stream, spots, preferred_element_type=F32)
    stream = placed[:width] + placed[width:]
    for r in range(levels):
        copies[r].wait()
        share = share_ref[r : r + 1, :]
        offset = off_ref[r : r + 1, :]
        heat = tv[r].T
        for k, weight in enumerate((share * (1.0 - offset), share * offset)):
            hi, lo = two_parts(heat * weight)
            twt[r, 2 * k * width : (2 * k + 1) * width, :] = hi
            twt[r, (2 * k + 1) * width : (2 * k + 2) * width, :] = lo

    def step(n, carry):
        total = jnp.zeros((4 * width, tile), F32)
        for r in range(levels):
            marks = one_hot(tile, n * tile, low_ref[r : r + 1, :])
            total = total + lax.dot_general(twt[r], marks, NT, preferred_element_type=F32)
        at = pl.ds(pl.multiple_of(n * tile, tile), tile)
        lower_sum[:, at] = total[:width] + total[width : 2 * width]
        upper_sum[:, at] = total[2 * width : 3 * width] + total[3 * width :]
        return carry

    lax.fori_loop(0, cells // tile, step, 0)
    zint = 0.25 * geo * (lower_sum[...] + pltpu.roll(upper_sum[...], 1, axis=1))
    zero = jnp.zeros((1, cells), F32)
    ahead = jnp.concatenate([zint[1:], zero], axis=0)
    behind = jnp.concatenate([zero, zint[:-1]], axis=0)
    partial = stream - (ahead - behind)
    sp_ref[...] = partial
    edge_ref[0] = jnp.concatenate([zint[:1], partial[:1]], axis=0)
    edge_ref[1] = jnp.concatenate([zint[-1:], partial[-1:]], axis=0)


def exchange_kernel(t_hbm, sp_ref, edge_ref, sall_ref, eall_ref, under_ref, over_ref, rim, ends, rim_send, rs_buf, rim_buf, own, rim_own, rs_send, rs_recv, e_send, e_recv, ag_send, ag_recv, ea_send, ea_recv, ma_send, ma_recv, h_send, h_recv):
    me = lax.axis_index("row")
    ma = lax.axis_index("ma")
    right, left = lax.rem(ma + 1, N_MA), lax.rem(ma + N_MA - 1, N_MA)
    cells = sp_ref.shape[2]
    levels, nodes = t_hbm.shape[:2]
    parts = h_send.shape[1]
    piece = nodes // parts

    barrier = pltpu.get_barrier_semaphore()
    for d in range(1, N_ROW):
        pl.semaphore_signal(barrier, inc=1, device_id={"row": lax.rem(me + d, N_ROW)}, device_id_type=MESH)
    for side in (left, right):
        pl.semaphore_signal(barrier, inc=1, device_id={"ma": side}, device_id_type=MESH)
    pl.semaphore_wait(barrier, N_ROW + 1)

    def to_row(src, dst, send, recv, peer):
        return pltpu.make_async_remote_copy(src_ref=src, dst_ref=dst, send_sem=send, recv_sem=recv, device_id={"row": peer}, device_id_type=MESH)

    def halo(side, k):
        peer = jnp.maximum(me - 1, 0) if side == 0 else jnp.minimum(me + 1, N_ROW - 1)
        at = pl.ds(k * piece, piece)
        return to_row(
            t_hbm.at[0 if side == 0 else levels - 1, at],
            (over_ref if side == 0 else under_ref).at[at],
            h_send.at[side, k],
            h_recv.at[side, k],
            peer,
        )

    def halo_start(first, last):
        for side, there in ((0, me > 0), (1, me < N_ROW - 1)):

            @pl.when(there)
            def _(side=side):
                for k in range(first, last):
                    halo(side, k).start()

    rims = [
        pltpu.make_async_remote_copy(src_ref=edge_ref.at[k], dst_ref=rim.at[k], send_sem=ma_send.at[k], recv_sem=ma_recv.at[k], device_id={"ma": side}, device_id_type=MESH)
        for k, side in enumerate((left, right))
    ]
    for copy in rims:
        copy.start()
    for d in range(1, N_ROW):
        peer = lax.rem(me + d, N_ROW)

        @pl.when(jnp.logical_and(peer > 0, peer < N_ROW - 1))
        def _(d=d, peer=peer):
            to_row(sp_ref.at[peer], rs_buf.at[d], rs_send.at[d], rs_recv.at[d], peer).start()

    for copy in rims:
        copy.wait()
    ends[0] = sp_ref[0]
    ends[1] = sp_ref[N_ROW - 1]
    ends[0, 0:1] = sp_ref[0, 0:1] + rim[1, 0:1]
    ends[1, 7:8] = sp_ref[N_ROW - 1, 7:8] - rim[0, 0:1]
    outer = (rim[1, 1:2] - edge_ref[0, 0:1], rim[0, 1:2] + edge_ref[1, 0:1])
    for p in range(N_ROW):
        at = p % 8
        rim_send[p] = outer[p // 8][:, at * 128 : (at + 1) * 128]
    for k, p in enumerate((0, N_ROW - 1)):

        @pl.when(me != p)
        def _(k=k, p=p):
            d = lax.rem(p - me + N_ROW, N_ROW)
            to_row(ends.at[k], rs_buf.at[d], rs_send.at[d], rs_recv.at[d], p).start()

    e_out = []
    for d in range(1, N_ROW):
        peer = lax.rem(me + d, N_ROW)
        e_out.append(to_row(rim_send.at[peer], rim_buf.at[d], e_send.at[d], e_recv.at[d], peer))
        e_out[-1].start()
    half = parts // 2
    halo_start(0, half)

    def rs_copy(d):
        return to_row(sp_ref.at[0], rs_buf.at[d], rs_send.at[d], rs_recv.at[d], lax.rem(me + d, N_ROW))

    total = jnp.where(me == 0, ends[0], jnp.where(me == N_ROW - 1, ends[1], sp_ref[me]))
    rim_total = rim_send[me]
    for d in range(1, N_ROW):
        rs_copy(d).wait_recv()
        total = total + rs_buf[d]
    for d in range(1, N_ROW):
        e_out[d - 1].wait_recv()
        rim_total = rim_total + rim_buf[d]
    own[...] = total
    rim_own[...] = rim_total
    sall_ref[me] = total
    eall_ref[me] = rim_total
    ag = []
    for d in range(1, N_ROW):
        peer = lax.rem(me + d, N_ROW)
        ag.append(to_row(own, sall_ref.at[me], ag_send.at[d], ag_recv.at[d], peer))
        ag.append(to_row(rim_own, eall_ref.at[me], ea_send.at[d], ea_recv.at[d], peer))
    for copy in ag:
        copy.start()
    halo_start(half, parts)
    for d in range(1, N_ROW):
        rs_copy(d).wait_send()
        e_out[d - 1].wait_send()
    for copy in ag:
        copy.wait()
    for side, there, comes in ((0, me > 0, me < N_ROW - 1), (1, me < N_ROW - 1, me > 0)):

        @pl.when(there)
        def _(side=side):
            for k in range(parts):
                halo(side, k).wait_send()

        @pl.when(comes)
        def _(side=side):
            for k in range(parts):
                halo(side, k).wait_recv()


def advance_kernel(t_hbm, under_hbm, over_hbm, low_ref, off_ref, holder_ref, stream_ref, sin_ref, cos_ref, sall_ref, eall_ref, out_hbm, flow_ref, tp, vel, out, sems, out_sems):
    levels, nodes, width = out.shape
    cells = holder_ref.shape[1]
    tile = 256
    me = lax.axis_index("row")
    body = pl.ds(8, nodes)
    sources = [under_hbm] + [t_hbm.at[r] for r in range(levels)] + [over_hbm]
    copies = [pltpu.make_async_copy(src, tp.at[r, body], sems.at[r]) for r, src in enumerate(sources)]
    for copy in copies:
        copy.start()
    for r in range(levels):
        tp[r + 1, 0:8] = jnp.zeros((8, width), F32)
        tp[r + 1, nodes + 8 : nodes + 16] = jnp.zeros((8, width), F32)
    stream = sall_ref[...].reshape(width, cells)
    spots = own_slots(holder_ref[...], me, stream_ref.shape[0])
    parts = jnp.concatenate(two_parts(stream), axis=0)
    held = lax.dot_general(parts, spots, NT, preferred_element_type=F32)
    held = (held[:width] + held[width:]).T
    count = jnp.sum((holder_ref[...] == me).astype(F32), axis=1, keepdims=True).astype(jnp.int32)
    slot = lax.broadcasted_iota(jnp.int32, held.shape, 0)
    flow_ref[...] = jnp.where(slot < count, held, stream_ref[...])

    first = jnp.concatenate([eall_ref[p] for p in range(8)], axis=1)
    last = jnp.concatenate([eall_ref[p] for p in range(8, 16)], axis=1)
    ahead = jnp.concatenate([stream[1:], last], axis=0)
    behind = jnp.concatenate([first, stream[:-1]], axis=0)
    velocity = (0.5 * geo_row(cells)) * (ahead - behind)
    change = pltpu.roll(velocity, cells - 1, axis=1) - velocity
    for k, x in enumerate(two_parts(velocity) + two_parts(change)):
        vel[k * width : (k + 1) * width, :] = x
    for copy in copies:
        copy.wait()

    @pl.when(me == 0)
    def _():
        tp[0, 8 : nodes + 8] = jnp.zeros((nodes, width), F32)

    @pl.when(me == N_ROW - 1)
    def _():
        tp[levels + 1, 8 : nodes + 8] = jnp.zeros((nodes, width), F32)

    def step(r, carry):
        for k in range(nodes // tile):
            at = slice(k * tile, (k + 1) * tile)
            marks = one_hot(cells, 0, low_ref[pl.ds(r, 1), at])
            both = jnp.dot(vel[...], marks, preferred_element_type=F32)
            drift = both[:width] + both[width : 2 * width]
            drift = drift + off_ref[pl.ds(r, 1), at] * (both[2 * width : 3 * width] + both[3 * width :])
            drift = drift.T
            lo, hi = 8 + k * tile, 8 + (k + 1) * tile
            radial = tp[r + 2, lo:hi] - tp[r, lo:hi]
            polar = tp[r + 1, lo + 1 : hi + 1] - tp[r + 1, lo - 1 : hi - 1]
            out[r, at] = tp[r + 1, lo:hi] - drift * (sin_ref[at] * radial + cos_ref[at] * polar)
        pltpu.make_async_copy(out.at[r], out_hbm.at[r], out_sems.at[r]).start()
        return carry

    lax.fori_loop(0, levels, step, 0)
    for r in range(levels):
        pltpu.make_async_copy(out.at[r], out_hbm.at[r], out_sems.at[r]).wait()


VMEM = pl.BlockSpec(memory_space=pltpu.VMEM)
ANY = pl.BlockSpec(memory_space=pl.ANY)
DMA = pltpu.SemaphoreType.DMA


def per_device(heat, lower, offset, share, holder, stream):
    levels, nodes, width = heat.shape
    cells = holder.shape[0]
    slots = stream.shape[0]
    holder = holder.reshape(1, cells)
    angle = math.pi * (np.arange(nodes, dtype=np.float32) + np.float32(0.5)) / nodes
    sines = jnp.asarray(np.repeat((0.125 * np.sin(angle)).astype(np.float32)[:, None], width, axis=1))
    cosines = jnp.asarray(np.repeat((0.125 * np.cos(angle)).astype(np.float32)[:, None], width, axis=1))
    params = functools.partial(pltpu.CompilerParams, vmem_limit_bytes=48 << 20)

    partial, edges = pl.pallas_call(
        integrate_kernel,
        out_shape=(jax.ShapeDtypeStruct((width, cells), F32), jax.ShapeDtypeStruct((2, 2, cells), F32)),
        in_specs=[ANY] + [VMEM] * 5,
        out_specs=(VMEM, VMEM),
        scratch_shapes=[
            pltpu.VMEM((levels, nodes, width), F32),
            pltpu.VMEM((levels, 4 * width, nodes), BF16),
            pltpu.VMEM((width, cells), F32),
            pltpu.VMEM((width, cells), F32),
            DMA((levels,)),
        ],
        compiler_params=params(),
        name="integrate",
    )(heat, lower, offset, share, holder, stream)

    rows = width // N_ROW
    parts = 6
    sem = lambda: DMA((N_ROW,))
    sall, eall, under, over = pl.pallas_call(
        exchange_kernel,
        out_shape=(
            jax.ShapeDtypeStruct((N_ROW, rows, cells), F32),
            jax.ShapeDtypeStruct((N_ROW, 1, 128), F32),
            jax.ShapeDtypeStruct((nodes, width), F32),
            jax.ShapeDtypeStruct((nodes, width), F32),
        ),
        in_specs=[ANY, VMEM, VMEM],
        out_specs=(VMEM, VMEM, ANY, ANY),
        scratch_shapes=[
            pltpu.VMEM((2, 2, cells), F32),
            pltpu.VMEM((2, rows, cells), F32),
            pltpu.VMEM((N_ROW, 1, 128), F32),
            pltpu.VMEM((N_ROW, rows, cells), F32),
            pltpu.VMEM((N_ROW, 1, 128), F32),
            pltpu.VMEM((rows, cells), F32),
            pltpu.VMEM((1, 128), F32),
            sem(), sem(), sem(), sem(), sem(), sem(), sem(), sem(),
            DMA((2,)), DMA((2,)), DMA((2, parts)), DMA((2, parts)),
        ],
        compiler_params=params(collective_id=0, has_side_effects=True),
        name="exchange",
    )(heat, partial.reshape(N_ROW, rows, cells), edges)

    return pl.pallas_call(
        advance_kernel,
        out_shape=(jax.ShapeDtypeStruct(heat.shape, F32), jax.ShapeDtypeStruct((slots, width), F32)),
        in_specs=[ANY] * 3 + [VMEM] * 8,
        out_specs=(ANY, VMEM),
        scratch_shapes=[
            pltpu.VMEM((levels + 2, nodes + 16, width), F32),
            pltpu.VMEM((4 * width, cells), BF16),
            pltpu.VMEM((levels, nodes, width), F32),
            DMA((levels + 2,)),
            DMA((levels,)),
        ],
        compiler_params=params(),
        name="advance",
    )(heat, under, over, lower, offset, holder, stream, sines, cosines, sall, eall)


def solution(mesh):
    return jax.shard_map(
        per_device,
        mesh=mesh,
        in_specs=(P("row", None, "ma"), P("row", None), P("row", None), P("row", None), P(), P("row", "ma")),
        out_specs=(P("row", None, "ma"), P("row", "ma")),
        check_vma=False,
    )
```

time: 243 us -> 75.1 us (0.31)
  the two profiles are of different devices: /device:TPU:2 before, /device:TPU:28 now
where the time goes in v1:
time: 75.1 us; the launch traced here: 74.7 us
  Pallas kernels  68.4 us (91%)
  local copies, waits for them, and re-layouts  5.63 us (7%)
    pallas_call x1, Pallas kernels, per_device(): pl.pallas_call(exchange_kernel, out_shape=(jax.ShapeDtypeStruct((N_ROW, r...  44.1 us
    pallas_call x1, Pallas kernels, per_device(): pl.pallas_call(advance_kernel, out_shape=(jax.ShapeDtypeStruct(heat.shape...  13.2 us
    pallas_call x1, Pallas kernels, per_device(): pl.pallas_call(integrate_kernel, out_shape=(jax.ShapeDtypeStruct((width,...  11.1 us
    unnamed x18, local copies, waits for them, and re-layouts  5.63 us

profile of v1, /device:TPU:28, one launch (start us, length us, event | category | flops | bytes accessed | tf_op | source)
XLA Modules:
  0.0 74.7 jit_solution(7312383427427018545)
XLA Ops:
  0.6 0.0 copy-start
  0.6 1.9 %copy-done = f32[8,768,128]{2,1,0:T(8,128)S(1)} copy-done((f32[8,768,128]{2,1,0:T(8,128)S(1)}, f32[8,768,128]{2,1,0:T(8,128)}, u32[]{:S(2)}) %copy-start) | copy-done | bytes 3145752
  2.5 0.0 copy-start.3
  2.5 0.8 %copy-done.3 = f32[128,128]{1,0:T(8,128)S(1)} copy-done((f32[128,128]{1,0:T(8,128)S(1)}, f32[128,128]{1,0:T(8,128)}, u32[]{:S(2)}) %copy-start.3) | copy-done | bytes 65560
  3.4 0.0 copy-start.5
  3.4 0.7 copy-done.5
  4.1 0.0 copy-start.6
  4.1 0.7 copy-done.6
  4.8 0.0 copy-start.7
  4.8 0.7 copy-done.7
  5.6 0.0 copy-start.8
  5.6 0.7 copy-done.8
  6.3 0.0 copy-start.1
  6.3 0.0 copy-start.2
  6.3 0.0 copy-start.4
  6.3 11.1 %integrate.1 = (f32[128,1024]{1,0:T(8,128)S(1)}, f32[2,2,1024]{2,1,0:T(2,128)S(1)}) custom-call(f32[8,768,128]{2,1,0:T(8,128)S(1)} %copy-done, s32[8,768]{1,0:T(8,128)S(1)} %copy-done.5, f32[8,768]{1,0:T(8,128)S(1)} %copy-done.6, f32[8,768]{1,0:T(8,128)S(1)} %copy-done.7, s32[1,1024]{1,0:T(1,128)S(1)} %bitcast.3, f32[128,128]{1,0:T(8,128)S(1)} %copy-done.3), custom_call_target="tpu_custom_call" | custom-call | tf_op jit(solution)/shard_map/integrate/pallas_call | solution.py:279
  17.4 44.1 %exchange.1 = (f32[16,8,1024]{2,1,0:T(8,128)S(1)}, f32[16,1,128]{2,1,0:T(1,128)S(1)}, f32[768,128]{1,0:T(8,128)S(1)}, f32[768,128]{1,0:T(8,128)S(1)}) custom-call(f32[8,768,128]{2,1,0:T(8,128)S(1)} %copy-done, f32[16,8,1024]{2,1,0:T(8,128)S(1)} %bitcast.2, f32[2,2,1024]{2,1,0:T(2,128)S(1)} %get-tuple-element.9.edge_ref), custom_call_target="tpu_custom_call" | custom-call | tf_op jit(solution)/shard_map/exchange/pallas_call | solution.py:298
  61.5 0.0 copy-done.1
  61.5 0.0 copy-done.2
  61.5 0.0 copy-done.4
  61.5 13.2 %advance.1 = (f32[8,768,128]{2,1,0:T(8,128)}, f32[128,128]{1,0:T(8,128)}) custom-call(f32[8,768,128]{2,1,0:T(8,128)S(1)} %copy-done, f32[768,128]{1,0:T(8,128)S(1)} %get-tuple-element.10.under_hbm, f32[768,128]{1,0:T(8,128)S(1)} %get-tuple-element.11.over_hbm, s32[8,768]{1,0:T(8,128)S(1)} %copy-done.5, f32[8,768]{1,0:T(8,128)S(1)} %copy-done.6, ...), custom_call_target="tpu_custom_call" | custom-call | tf_op jit(solution)/shard_map/advance/pallas_call | solution.py:323
Async XLA Ops:
  0.6 1.9 %copy-start = (f32[8,768,128]{2,1,0:T(8,128)S(1)}, f32[8,768,128]{2,1,0:T(8,128)}, u32[]{:S(2)}) copy-start(f32[8,768,128]{2,1,0:T(8,128)} %t_hbm.5) | copy-start | bytes 9437188
  2.5 0.8 %copy-start.3 = (f32[128,128]{1,0:T(8,128)S(1)}, f32[128,128]{1,0:T(8,128)}, u32[]{:S(2)}) copy-start(f32[128,128]{1,0:T(8,128)} %stream_ref.3) | copy-start | bytes 196612
  3.4 0.7 copy-start.5
  4.1 0.7 copy-start.6
  4.8 0.7 copy-start.7
  5.6 0.7 copy-start.8
  6.3 55.2 %copy-start.1 = (f32[768,128]{1,0:T(8,128)S(1)}, f32[768,128]{1,0:T(8,128)}, u32[]{:S(2)}) copy-start(f32[768,128]{1,0:T(8,128)} %constant.5.clone.cos_ref) | copy-start | bytes 1179652
  6.3 55.2 %copy-start.2 = (f32[768,128]{1,0:T(8,128)S(1)}, f32[768,128]{1,0:T(8,128)}, u32[]{:S(2)}) copy-start(f32[768,128]{1,0:T(8,128)} %constant.4.clone.sin_ref) | copy-start | bytes 1179652
  6.3 55.2 %copy-start.4 = (f32[128,128]{1,0:T(8,128)S(1)}, f32[128,128]{1,0:T(8,128)}, u32[]{:S(2)}) copy-start(f32[128,128]{1,0:T(8,128)} %stream_ref.3) | copy-start | bytes 196612

commit v2 on v0

v2 whole, which is shorter than its diff:
```python
import functools
import math

import jax
import jax.numpy as jnp
import numpy as np
from jax import lax
from jax.experimental import pallas as pl
from jax.experimental.pallas import tpu as pltpu
from jax.sharding import PartitionSpec as P

MESH = pl.DeviceIdType.MESH
F32 = jnp.float32
BF16 = jnp.bfloat16
N_ROW = 16
N_MA = 16
NT = (((1,), (1,)), ((), ()))


def two_parts(x):
    hi = x.astype(BF16)
    return hi, (x - hi.astype(F32)).astype(BF16)


def one_hot(rows, first, index):
    at = lax.broadcasted_iota(jnp.int32, (rows, index.shape[1]), 0)
    return jnp.where(at == index - first, 1.0, 0.0).astype(BF16)


def geo_row(cells, first, count):
    c = (first + lax.broadcasted_iota(jnp.int32, (1, count), 1)).astype(F32)
    return 1.0 / (0.25 + (c + 0.5) / cells)


def own_slots(holder, me, slots):
    cells = holder.shape[1]
    start = jnp.sum((holder < me).astype(F32), axis=1, keepdims=True).astype(jnp.int32)
    c = lax.broadcasted_iota(jnp.int32, (1, cells), 1)
    return one_hot(slots, 0, jnp.where(holder == me, c - start, -1))


def fused_kernel(
    t_hbm, low_hbm, off_hbm, share_hbm, holder_hbm, stream_hbm,
    tv, pvt, vel_last, sall,
    low, off, share, holder, stream_in, stream, twt, sp, edge, rim, ends, rim_send, rs_buf, rim_buf, own, rim_own, eall, carry_up, carry_vel, vel,
    t_sem, in_sem, rs_send, rs_recv, ag_send, ag_recv, e_send, e_recv, ea_send, ea_recv, ma_send, ma_recv, h_send, h_recv,
):
    levels, width, nodes = pvt.shape
    cells = holder.shape[1]
    stages, tile = sp.shape[0], sp.shape[3]
    me = lax.axis_index("row")
    ma = lax.axis_index("ma")
    right, left = lax.rem(ma + 1, N_MA), lax.rem(ma + N_MA - 1, N_MA)
    parts = h_send.shape[1]
    piece = nodes // parts

    small = [(holder_hbm, holder), (stream_hbm, stream_in), (share_hbm, share), (off_hbm, off), (low_hbm, low)]
    loads = [pltpu.make_async_copy(src, dst, in_sem.at[k]) for k, (src, dst) in enumerate(small)]
    heat_loads = [pltpu.make_async_copy(t_hbm.at[r], tv.at[r + 1], t_sem.at[r]) for r in range(levels)]
    for copy in loads + heat_loads:
        copy.start()
    barrier = pltpu.get_barrier_semaphore()
    for d in range(1, N_ROW):
        pl.semaphore_signal(barrier, inc=1, device_id={"row": lax.rem(me + d, N_ROW)}, device_id_type=MESH)
    for side in (left, right):
        pl.semaphore_signal(barrier, inc=1, device_id={"ma": side}, device_id_type=MESH)

    @pl.when(me == 0)
    def _():
        tv[0] = jnp.zeros((nodes, width), F32)

    @pl.when(me == N_ROW - 1)
    def _():
        tv[levels + 1] = jnp.zeros((nodes, width), F32)

    for copy in loads:
        copy.wait()
    spots = own_slots(holder[...], me, stream_in.shape[0])
    placed = jnp.dot(jnp.concatenate(two_parts(stream_in[...].T), axis=0), spots, preferred_element_type=F32)
    stream[...] = placed[:width] + placed[width:]
    for r in range(levels):
        heat_loads[r].wait()
        weights = share[r : r + 1, :]
        offset = off[r : r + 1, :]
        heat = tv[r + 1].T
        for k, weight in enumerate((weights * (1.0 - offset), weights * offset)):
            hi, lo = two_parts(heat * weight)
            twt[r, 2 * k * width : (2 * k + 1) * width, :] = hi
            twt[r, (2 * k + 1) * width : (2 * k + 2) * width, :] = lo

    pl.semaphore_wait(barrier, N_ROW + 1)

    def to_row(src, dst, send, recv, peer):
        return pltpu.make_async_remote_copy(src_ref=src, dst_ref=dst, send_sem=send, recv_sem=recv, device_id={"row": peer}, device_id_type=MESH)

    def halo(side, k):
        peer = jnp.maximum(me - 1, 0) if side == 0 else jnp.minimum(me + 1, N_ROW - 1)
        at = pl.ds(k * piece, piece)
        mine, theirs = (1, levels + 1) if side == 0 else (levels, 0)
        return to_row(tv.at[mine, at], tv.at[theirs, at], h_send.at[side, k], h_recv.at[side, k], peer)

    def halo_start(first, last):
        for side, there in ((0, me > 0), (1, me < N_ROW - 1)):

            @pl.when(there)
            def _(side=side):
                for k in range(first, last):
                    halo(side, k).start()

    def pieces(n):
        return (2 * n, 2 * n + 1, 8 + 2 * n, 8 + 2 * n + 1)

    def rim_copies(n):
        return [
            pltpu.make_async_remote_copy(src_ref=edge.at[n, k], dst_ref=rim.at[n, k], send_sem=ma_send.at[n, k], recv_sem=ma_recv.at[n, k], device_id={"ma": side}, device_id_type=MESH)
            for k, side in enumerate((left, right))
        ]

    def rs_copy(n, d, src):
        return to_row(src, rs_buf.at[n, d], rs_send.at[n, d], rs_recv.at[n, d], lax.rem(me + d, N_ROW))

    def ag_copy(n, d):
        return to_row(own.at[n], sall.at[n, me], ag_send.at[n, d], ag_recv.at[n, d], lax.rem(me + d, N_ROW))

    def e_copy(p, d):
        return to_row(rim_send.at[p], rim_buf.at[d], e_send.at[d], e_recv.at[d], p)

    def ea_copy(d):
        return to_row(rim_own, eall.at[me], ea_send.at[d], ea_recv.at[me], lax.rem(me + d, N_ROW))

    def sum_columns(n):
        total = jnp.zeros((4 * width, tile), F32)
        for r in range(levels):
            marks = one_hot(tile, n * tile, low[r : r + 1, :])
            total = total + lax.dot_general(twt[r], marks, NT, preferred_element_type=F32)
        lower = total[:width] + total[width : 2 * width]
        upper = pltpu.roll(total[2 * width : 3 * width] + total[3 * width :], 1, axis=1)
        lane = lax.broadcasted_iota(jnp.int32, (width, 128), 1)
        before = jnp.zeros((width, 128), F32) if n == 0 else carry_up[...]
        carry_up[...] = upper[:, :128]
        upper = jnp.concatenate([jnp.where(lane == 0, before, upper[:, :128]), upper[:, 128:]], axis=1)
        zint = (0.25 * geo_row(cells, n * tile, tile)) * (lower + upper)
        zero = jnp.zeros((1, tile), F32)
        ahead = jnp.concatenate([zint[1:], zero], axis=0)
        behind = jnp.concatenate([zero, zint[:-1]], axis=0)
        partial = stream[:, n * tile : (n + 1) * tile] - (ahead - behind)
        sp[n] = partial.reshape(N_ROW, width // N_ROW, tile)
        edge[n, 0] = jnp.concatenate([zint[:1], partial[:1]], axis=0)
        edge[n, 1] = jnp.concatenate([zint[-1:], partial[-1:]], axis=0)

    def send_inner(n):
        for copy in rim_copies(n):
            copy.start()
        for d in range(1, N_ROW):
            peer = lax.rem(me + d, N_ROW)

            @pl.when(jnp.logical_and(peer > 0, peer < N_ROW - 1))
            def _(d=d, peer=peer):
                rs_copy(n, d, sp.at[n, peer]).start()

    def send_outer(n):
        for copy in rim_copies(n):
            copy.wait()
        last = width // N_ROW - 1
        ends[n, 0] = sp[n, 0]
        ends[n, 1] = sp[n, N_ROW - 1]
        ends[n, 0, 0:1] = sp[n, 0, 0:1] + rim[n, 1, 0:1]
        ends[n, 1, last : last + 1] = sp[n, N_ROW - 1, last : last + 1] - rim[n, 0, 0:1]
        outer = (rim[n, 1, 1:2] - edge[n, 0, 0:1], rim[n, 0, 1:2] + edge[n, 1, 0:1])
        for i, p in enumerate(pieces(n)):
            rim_send[p] = outer[i // 2][:, (i % 2) * 128 : (i % 2 + 1) * 128]
        for k, p in enumerate((0, N_ROW - 1)):

            @pl.when(me != p)
            def _(k=k, p=p):
                rs_copy(n, lax.rem(p - me + N_ROW, N_ROW), ends.at[n, k]).start()

        for p in pieces(n):

            @pl.when(me != p)
            def _(p=p):
                e_copy(p, lax.rem(p - me + N_ROW, N_ROW)).start()

    def reduce_rows(n):
        total = jnp.where(me == 0, ends[n, 0], jnp.where(me == N_ROW - 1, ends[n, 1], sp[n, me]))
        for d in range(1, N_ROW):
            rs_copy(n, d, own.at[n]).wait_recv()
            total = total + rs_buf[n, d]
        own[n] = total
        sall[n, me] = total
        for d in range(1, N_ROW):
            ag_copy(n, d).start()

        @pl.when(lax.rem(me, 8) // 2 == n)
        def _():
            total = rim_send[me]
            for d in range(1, N_ROW):
                e_copy(0, d).wait_recv()
                total = total + rim_buf[d]
            rim_own[...] = total
            eall[me] = total
            for d in range(1, N_ROW):
                ea_copy(d).start()

    def velocity(n):
        for d in range(1, N_ROW):
            ag_copy(n, d).wait_recv()
        for p in pieces(n):

            @pl.when(me != p)
            def _(p=p):
                to_row(rim_own, eall.at[p], ea_send.at[0], ea_recv.at[p], p).wait_recv()

        field = sall[n].reshape(width, tile)
        first, last = (jnp.concatenate([eall[p], eall[p + 1]], axis=1) for p in (2 * n, 8 + 2 * n))
        ahead = jnp.concatenate([field[1:], last], axis=0)
        behind = jnp.concatenate([first, field[:-1]], axis=0)
        now = (0.5 * geo_row(cells, n * tile, tile)) * (ahead - behind)
        lane = lax.broadcasted_iota(jnp.int32, (width, 128), 1)
        down = pltpu.roll(now, 1, axis=1)
        before = jnp.zeros((width, 128), F32) if n == 0 else carry_vel[...]
        carry_vel[...] = down[:, :128]
        down = jnp.concatenate([jnp.where(lane == 0, before, down[:, :128]), down[:, 128:]], axis=1)
        into = vel_last if n == stages - 1 else vel
        for k, x in enumerate(two_parts(down) + two_parts(now - down)):
            into[k * width : (k + 1) * width, :] = x

    def interpolate(n):
        def step(r, carry):
            for k in range(nodes // 256):
                at = slice(k * 256, (k + 1) * 256)
                marks = one_hot(tile, n * tile - 1, low[pl.ds(r, 1), at])
                both = jnp.dot(vel[...], marks, preferred_element_type=F32)
                part = both[:width] + both[width : 2 * width]
                part = part + off[pl.ds(r, 1), at] * (both[2 * width : 3 * width] + both[3 * width :])
                pvt[r, :, at] = part if n == 0 else pvt[r, :, at] + part
            return carry

        lax.fori_loop(0, levels, step, 0)

    halo_start(0, 2)
    for n in range(stages):
        sum_columns(n)
        send_inner(n)
        if n > 0:
            send_outer(n - 1)
        halo_start(n + 2, n + 3)
    send_outer(stages - 1)
    for n in range(stages):
        reduce_rows(n)
        halo_start(n + 6, n + 7)
    halo_start(10, parts)
    for n in range(stages):
        velocity(n)
        if n < stages - 1:
            interpolate(n)
    for n in range(stages):
        for d in range(1, N_ROW):
            rs_copy(n, d, own.at[n]).wait_send()
            ag_copy(n, d).wait_send()
    for d in range(1, N_ROW):
        e_copy(0, d).wait_send()
        ea_copy(d).wait_send()
    for side, there, comes in ((0, me > 0, me < N_ROW - 1), (1, me < N_ROW - 1, me > 0)):

        @pl.when(there)
        def _(side=side):
            for k in range(parts):
                halo(side, k).wait_send()

        @pl.when(comes)
        def _(side=side):
            for k in range(parts):
                halo(side, k).wait_recv()


def advance_kernel(tv, pvt, vel, sall, low, off, holder, stream, sines, cosines, out_hbm, flow, out, out_sem):
    levels, nodes, width = out.shape
    cells = holder.shape[1]
    stages, tile = sall.shape[0], sall.shape[3]
    me = lax.axis_index("row")

    def step(r, carry):
        for k in range(nodes // 256):
            lo, hi = k * 256, (k + 1) * 256
            at = slice(lo, hi)
            marks = one_hot(tile, (stages - 1) * tile - 1, low[pl.ds(r, 1), at])
            both = jnp.dot(vel[...], marks, preferred_element_type=F32)
            drift = pvt[r, :, at] + both[:width] + both[width : 2 * width]
            drift = drift + off[pl.ds(r, 1), at] * (both[2 * width : 3 * width] + both[3 * width :])
            drift = drift.T
            zero = jnp.zeros((1, width), F32)
            south = jnp.concatenate([tv[r + 1, lo + 1 : hi], zero], axis=0) if hi == nodes else tv[r + 1, lo + 1 : hi + 1]
            north = jnp.concatenate([zero, tv[r + 1, lo : hi - 1]], axis=0) if lo == 0 else tv[r + 1, lo - 1 : hi - 1]
            radial = tv[r + 2, at] - tv[r, at]
            out[r, at] = tv[r + 1, at] - drift * (sines[at] * radial + cosines[at] * (south - north))
        pltpu.make_async_copy(out.at[r], out_hbm.at[r], out_sem.at[r]).start()
        return carry

    lax.fori_loop(0, levels, step, 0)
    spots = own_slots(holder[...], me, stream.shape[0])
    held = jnp.zeros((2 * width, stream.shape[0]), F32)
    for n in range(stages):
        field = jnp.concatenate(two_parts(sall[n].reshape(width, tile)), axis=0)
        held = held + lax.dot_general(field, spots[:, n * tile : (n + 1) * tile], NT, preferred_element_type=F32)
    held = (held[:width] + held[width:]).T
    count = jnp.sum((holder[...] == me).astype(F32), axis=1, keepdims=True).astype(jnp.int32)
    slot = lax.broadcasted_iota(jnp.int32, held.shape, 0)
    flow[...] = jnp.where(slot < count, held, stream[...])
    for r in range(levels):
        pltpu.make_async_copy(out.at[r], out_hbm.at[r], out_sem.at[r]).wait()


VMEM = pl.BlockSpec(memory_space=pltpu.VMEM)
HBM = pl.BlockSpec(memory_space=pltpu.HBM)
DMA = pltpu.SemaphoreType.DMA


def per_device(heat, lower, offset, share, holder, stream):
    levels, nodes, width = heat.shape
    cells = holder.shape[0]
    slots = stream.shape[0]
    holder = holder.reshape(1, cells)
    angle = math.pi * (np.arange(nodes, dtype=np.float32) + np.float32(0.5)) / nodes
    sines = jnp.asarray(np.repeat((0.125 * np.sin(angle)).astype(np.float32)[:, None], width, axis=1))
    cosines = jnp.asarray(np.repeat((0.125 * np.cos(angle)).astype(np.float32)[:, None], width, axis=1))
    params = functools.partial(pltpu.CompilerParams, vmem_limit_bytes=40 << 20)

    rows = width // N_ROW
    parts = 12
    stages = 4
    tile = cells // stages
    both = lambda: DMA((stages, N_ROW))
    tv, pvt, vel, sall = pl.pallas_call(
        fused_kernel,
        out_shape=(
            jax.ShapeDtypeStruct((levels + 2, nodes, width), F32),
            jax.ShapeDtypeStruct((levels, width, nodes), F32),
            jax.ShapeDtypeStruct((4 * width, tile), BF16),
            jax.ShapeDtypeStruct((stages, N_ROW, rows, tile), F32),
        ),
        in_specs=[HBM] * 6,
        out_specs=(VMEM,) * 4,
        scratch_shapes=[
            pltpu.VMEM((levels, nodes), jnp.int32),
            pltpu.VMEM((levels, nodes), F32),
            pltpu.VMEM((levels, nodes), F32),
            pltpu.VMEM((1, cells), jnp.int32),
            pltpu.VMEM((slots, width), F32),
            pltpu.VMEM((width, cells), F32),
            pltpu.VMEM((levels, 4 * width, nodes), BF16),
            pltpu.VMEM((stages, N_ROW, rows, tile), F32),
            pltpu.VMEM((stages, 2, 2, tile), F32),
            pltpu.VMEM((stages, 2, 2, tile), F32),
            pltpu.VMEM((stages, 2, rows, tile), F32),
            pltpu.VMEM((N_ROW, 1, 128), F32),
            pltpu.VMEM((stages, N_ROW, rows, tile), F32),
            pltpu.VMEM((N_ROW, 1, 128), F32),
            pltpu.VMEM((stages, rows, tile), F32),
            pltpu.VMEM((1, 128), F32),
            pltpu.VMEM((N_ROW, 1, 128), F32),
            pltpu.VMEM((width, 128), F32),
            pltpu.VMEM((width, 128), F32),
            pltpu.VMEM((4 * width, tile), BF16),
            DMA((levels,)), DMA((5,)),
            both(), both(), both(), both(),
            DMA((N_ROW,)), DMA((N_ROW,)), DMA((N_ROW,)), DMA((N_ROW,)),
            DMA((stages, 2)), DMA((stages, 2)), DMA((2, parts)), DMA((2, parts)),
        ],
        compiler_params=params(collective_id=0, has_side_effects=True),
        name="columns",
    )(*(pltpu.with_memory_space_constraint(x, pltpu.HBM) for x in (heat, lower, offset, share, holder, stream)))

    return pl.pallas_call(
        advance_kernel,
        out_shape=(jax.ShapeDtypeStruct(heat.shape, F32), jax.ShapeDtypeStruct((slots, width), F32)),
        in_specs=[VMEM] * 10,
        out_specs=(HBM, VMEM),
        scratch_shapes=[pltpu.VMEM((levels, nodes, width), F32), DMA((levels,))],
        compiler_params=params(),
        name="advance",
    )(tv, pvt, vel, sall, lower, offset, holder, stream, sines, cosines)


def solution(mesh):
    return jax.shard_map(
        per_device,
        mesh=mesh,
        in_specs=(P("row", None, "ma"), P("row", None), P("row", None), P("row", None), P(), P("row", "ma")),
        out_specs=(P("row", None, "ma"), P("row", "ma")),
        check_vma=False,
    )
```

time: 243 us -> 56.9 us (0.23); the launches traced: 240 us -> 56.8 us
  matrix products: 97.9 us -> 0 us
  waiting for transfers between devices: 59.7 us -> 0 us
  Pallas kernels: 0 us -> 56.1 us
  local copies, waits for them, and re-layouts: 54.1 us -> 0.03 us
  starting transfers between devices: 24.2 us -> 0 us
  other arithmetic: 3.57 us -> 0 us
    dot_general x2 -> x0, matrix products: 97.9 us -> none  [the longest x1 52.1 us: per_device(): jnp.dot(interp, piece, precision=lax.Precision.HIGHEST, preferred_element...]
    pallas_call x0 -> x2, Pallas kernels: none -> 56.1 us  [the longest x1 50.3 us: per_device(): pl.pallas_call(fused_kernel, out_shape=(jax.ShapeDtypeStruct((levels + 2,...]
    gather x2 -> x0, local copies, waits for them, and re-layouts: 49.6 us -> none  [the longest x1 24.8 us: per_device(): slot_low = slot_of_cell[lower_cell]]
    all_to_all x2 -> x0, waiting for transfers between devices: 30 us -> none  [the longest x1 30 us: sum_at_owner(): lax.all_to_all(parts, axis, split_axis=0, concat_axis=0, tiled=True)]
    ppermute x4 -> x0, waiting for transfers between devices: 29.7 us -> none  [the longest x2 21.5 us: extended(): before = lax.ppermute(last, axis, up)]
    all_to_all x2 -> x0, starting transfers between devices: 15 us -> none  [the longest x1 11.3 us: sum_at_owner(): lax.all_to_all(parts, axis, split_axis=0, concat_axis=0, tiled=True)]
    ppermute x4 -> x0, starting transfers between devices: 9.18 us -> none  [the longest x2 6.16 us: extended(): before = lax.ppermute(last, axis, up)]
  transfers between devices with their start and end apart: 6 -> 0, of which waited for: 4 -> 0; matrix products, arithmetic and copies ran while one was open for 1% -> 0% of each run, Pallas kernels for 0% -> 0%
where the time goes in v2:
time: 56.9 us; the launch traced here: 56.8 us
  Pallas kernels  56.1 us (99%)
  between operations  0.73 us (1%)
    pallas_call x1, Pallas kernels, per_device(): pl.pallas_call(fused_kernel, out_shape=(jax.ShapeDtypeStruct((levels + 2,...  50.3 us
    pallas_call x1, Pallas kernels, per_device(): pl.pallas_call(advance_kernel, out_shape=(jax.ShapeDtypeStruct(heat.shape...  5.8 us

profile of v2, /device:TPU:2, one launch (start us, length us, event | category | flops | bytes accessed | tf_op | source)
XLA Modules:
  0.0 56.8 jit_solution(9644063811081361610)
XLA Ops:
  0.6 0.0 copy-start
  0.6 0.0 copy-start.1
  0.7 0.0 copy-start.2
  0.7 0.0 copy-start.4
  0.7 0.0 copy-start.3
  0.7 0.0 copy-start.5
  0.7 50.3 %columns.1 = (f32[10,768,128]{2,1,0:T(8,128)S(1)}, f32[8,128,768]{2,1,0:T(8,128)S(1)}, bf16[512,256]{1,0:T(8,128)(2,1)S(1)}, f32[4,16,8,256]{3,2,1,0:T(8,128)S(1)}) custom-call(f32[8,768,128]{2,1,0:T(8,128)} %t_hbm.1, s32[8,768]{1,0:T(8,128)} %low.1, f32[8,768]{1,0:T(8,128)} %off.1, f32[8,768]{1,0:T(8,128)} %share_hbm.1, s32[1,1024]{1,0:T(1,128)} %bitcast.1, ...), custom_call_target="tpu_custom_call" | custom-call | tf_op jit(solution)/shard_map/columns/pallas_call | solution.py:334
  51.0 0.0 copy-done
  51.0 0.0 copy-done.1
  51.0 0.0 copy-done.2
  51.0 0.0 copy-done.4
  51.0 0.0 copy-done.3
  51.0 0.0 copy-done.5
  51.0 5.8 %advance.1 = (f32[8,768,128]{2,1,0:T(8,128)}, f32[128,128]{1,0:T(8,128)}) custom-call(f32[10,768,128]{2,1,0:T(8,128)S(1)} %get-tuple-element.6.tv, f32[8,128,768]{2,1,0:T(8,128)S(1)} %get-tuple-element.7.pvt, bf16[512,256]{1,0:T(8,128)(2,1)S(1)} %get-tuple-element.8.vel, f32[4,16,8,256]{3,2,1,0:T(8,128)S(1)} %get-tuple-element.9.sall, ...), custom_call_target="tpu_custom_call" | custom-call | tf_op jit(solution)/shard_map/advance/pallas_call | solution.py:374
Async XLA Ops:
  0.6 50.4 %copy-start = (f32[768,128]{1,0:T(8,128)S(1)}, f32[768,128]{1,0:T(8,128)}, u32[]{:S(2)}) copy-start(f32[768,128]{1,0:T(8,128)} %constant.5.clone.cosines) | copy-start | bytes 1179652
  0.6 50.3 %copy-start.1 = (f32[768,128]{1,0:T(8,128)S(1)}, f32[768,128]{1,0:T(8,128)}, u32[]{:S(2)}) copy-start(f32[768,128]{1,0:T(8,128)} %constant.4.clone.sines) | copy-start | bytes 1179652
  0.7 50.3 %copy-start.2 = (f32[128,128]{1,0:T(8,128)S(1)}, f32[128,128]{1,0:T(8,128)}, u32[]{:S(2)}) copy-start(f32[128,128]{1,0:T(8,128)} %stream.1) | copy-start | bytes 196612
  0.7 50.3 %copy-start.4 = (f32[8,768]{1,0:T(8,128)S(1)}, f32[8,768]{1,0:T(8,128)}, u32[]{:S(2)}) copy-start(f32[8,768]{1,0:T(8,128)} %off.1) | copy-start | bytes 73732
  0.7 50.3 %copy-start.3 = (s32[8,768]{1,0:T(8,128)S(1)}, s32[8,768]{1,0:T(8,128)}, u32[]{:S(2)}) copy-start(s32[8,768]{1,0:T(8,128)} %low.1) | copy-start | bytes 73732
  0.7 50.3 %copy-start.5 = (s32[1024]{0:T(1024)S(1)}, s32[1024]{0:T(1024)}, u32[]{:S(2)}) copy-start(s32[1024]{0:T(1024)} %param.12) | copy-start | bytes 12292

commit v3 on v2

--- a/solution.py
+++ b/solution.py
@@ -14,6 +14,7 @@
 BF16 = jnp.bfloat16
 N_ROW = 16
 N_MA = 16
+HALO_PLAN = (2, 3, 4, 5, 6, 7, 8, 9, 10, 12)
 NT = (((1,), (1,)), ((), ()))
 
 
@@ -40,9 +41,9 @@
 
 
 def fused_kernel(
-    t_hbm, low_hbm, off_hbm, share_hbm, holder_hbm, stream_hbm,
-    tv, pvt, vel_last, sall,
-    low, off, share, holder, stream_in, stream, twt, sp, edge, rim, ends, rim_send, rs_buf, rim_buf, own, rim_own, eall, carry_up, carry_vel, vel,
+    t_hbm, low_hbm, off_hbm, share_hbm, holder_hbm, stream_hbm, sin_hbm, cos_hbm,
+    tv, pvt, vel_last, sall, slope,
+    sines, cosines, low, off, share, holder, stream_in, stream, twt, sp, edge, rim, ends, rim_send, rs_buf, rim_buf, own, rim_own, eall, carry_up, carry_vel, vel,
     t_sem, in_sem, rs_send, rs_recv, ag_send, ag_recv, e_send, e_recv, ea_send, ea_recv, ma_send, ma_recv, h_send, h_recv,
 ):
     levels, width, nodes = pvt.shape
@@ -51,10 +52,10 @@
     me = lax.axis_index("row")
     ma = lax.axis_index("ma")
     right, left = lax.rem(ma + 1, N_MA), lax.rem(ma + N_MA - 1, N_MA)
-    parts = h_send.shape[1]
+    parts = HALO_PLAN[-1]
     piece = nodes // parts
 
-    small = [(holder_hbm, holder), (stream_hbm, stream_in), (share_hbm, share), (off_hbm, off), (low_hbm, low)]
+    small = [(holder_hbm, holder), (stream_hbm, stream_in), (share_hbm, share), (off_hbm, off), (low_hbm, low), (sin_hbm, sines), (cos_hbm, cosines)]
     loads = [pltpu.make_async_copy(src, dst, in_sem.at[k]) for k, (src, dst) in enumerate(small)]
     heat_loads = [pltpu.make_async_copy(t_hbm.at[r], tv.at[r + 1], t_sem.at[r]) for r in range(levels)]
     for copy in loads + heat_loads:
@@ -73,7 +74,7 @@
     def _():
         tv[levels + 1] = jnp.zeros((nodes, width), F32)
 
-    for copy in loads:
+    for copy in loads[:5]:
         copy.wait()
     spots = own_slots(holder[...], me, stream_in.shape[0])
     placed = jnp.dot(jnp.concatenate(two_parts(stream_in[...].T), axis=0), spots, preferred_element_type=F32)
@@ -93,11 +94,14 @@
     def to_row(src, dst, send, recv, peer):
         return pltpu.make_async_remote_copy(src_ref=src, dst_ref=dst, send_sem=send, recv_sem=recv, device_id={"row": peer}, device_id_type=MESH)
 
+    def await_all(like, sem):
+        pltpu.make_async_copy(like, like, sem).wait()
+
     def halo(side, k):
         peer = jnp.maximum(me - 1, 0) if side == 0 else jnp.minimum(me + 1, N_ROW - 1)
         at = pl.ds(k * piece, piece)
         mine, theirs = (1, levels + 1) if side == 0 else (levels, 0)
-        return to_row(tv.at[mine, at], tv.at[theirs, at], h_send.at[side, k], h_recv.at[side, k], peer)
+        return to_row(tv.at[mine, at], tv.at[theirs, at], h_send.at[side], h_recv.at[side], peer)
 
     def halo_start(first, last):
         for side, there in ((0, me > 0), (1, me < N_ROW - 1)):
@@ -117,29 +121,33 @@
         ]
 
     def rs_copy(n, d, src):
-        return to_row(src, rs_buf.at[n, d], rs_send.at[n, d], rs_recv.at[n, d], lax.rem(me + d, N_ROW))
+        return to_row(src, rs_buf.at[n, d], rs_send, rs_recv.at[n], lax.rem(me + d, N_ROW))
 
     def ag_copy(n, d):
-        return to_row(own.at[n], sall.at[n, me], ag_send.at[n, d], ag_recv.at[n, d], lax.rem(me + d, N_ROW))
+        return to_row(own.at[n], sall.at[n, me], ag_send, ag_recv.at[n], lax.rem(me + d, N_ROW))
 
     def e_copy(p, d):
-        return to_row(rim_send.at[p], rim_buf.at[d], e_send.at[d], e_recv.at[d], p)
+        return to_row(rim_send.at[p], rim_buf.at[d], e_send, e_recv, p)
 
     def ea_copy(d):
-        return to_row(rim_own, eall.at[me], ea_send.at[d], ea_recv.at[me], lax.rem(me + d, N_ROW))
+        return to_row(rim_own, eall.at[me], ea_send, ea_recv.at[lax.rem(me, 8) // 2], lax.rem(me + d, N_ROW))
 
     def sum_columns(n):
-        total = jnp.zeros((4 * width, tile), F32)
+        sums = [jnp.zeros((4 * width, tile), F32)] * 2
         for r in range(levels):
             marks = one_hot(tile, n * tile, low[r : r + 1, :])
-            total = total + lax.dot_general(twt[r], marks, NT, preferred_element_type=F32)
-        lower = total[:width] + total[width : 2 * width]
-        upper = pltpu.roll(total[2 * width : 3 * width] + total[3 * width :], 1, axis=1)
+            sums[r % 2] = sums[r % 2] + lax.dot_general(twt[r], marks, NT, preferred_element_type=F32)
+        half = 2 * width
+        here, following = (0.25 * geo_row(cells, n * tile + k, tile) for k in range(2))
+        lower = here * sums[0][:half] + here * sums[1][:half]
+        lower = lower[:width] + lower[width:]
+        upper = following * sums[0][half:] + following * sums[1][half:]
+        upper = pltpu.roll(upper[:width] + upper[width:], 1, axis=1)
         lane = lax.broadcasted_iota(jnp.int32, (width, 128), 1)
         before = jnp.zeros((width, 128), F32) if n == 0 else carry_up[...]
         carry_up[...] = upper[:, :128]
         upper = jnp.concatenate([jnp.where(lane == 0, before, upper[:, :128]), upper[:, 128:]], axis=1)
-        zint = (0.25 * geo_row(cells, n * tile, tile)) * (lower + upper)
+        zint = lower + upper
         zero = jnp.zeros((1, tile), F32)
         ahead = jnp.concatenate([zint[1:], zero], axis=0)
         behind = jnp.concatenate([zero, zint[:-1]], axis=0)
@@ -183,8 +191,8 @@
 
     def reduce_rows(n):
         total = jnp.where(me == 0, ends[n, 0], jnp.where(me == N_ROW - 1, ends[n, 1], sp[n, me]))
+        await_all(rs_buf.at[n, pl.ds(1, N_ROW - 1)], rs_recv.at[n])
         for d in range(1, N_ROW):
-            rs_copy(n, d, own.at[n]).wait_recv()
             total = total + rs_buf[n, d]
         own[n] = total
         sall[n, me] = total
@@ -194,8 +202,8 @@
         @pl.when(lax.rem(me, 8) // 2 == n)
         def _():
             total = rim_send[me]
+            await_all(rim_buf.at[pl.ds(1, N_ROW - 1)], e_recv)
             for d in range(1, N_ROW):
-                e_copy(0, d).wait_recv()
                 total = total + rim_buf[d]
             rim_own[...] = total
             eall[me] = total
@@ -203,13 +211,13 @@
                 ea_copy(d).start()
 
     def velocity(n):
-        for d in range(1, N_ROW):
-            ag_copy(n, d).wait_recv()
-        for p in pieces(n):
-
-            @pl.when(me != p)
-            def _(p=p):
-                to_row(rim_own, eall.at[p], ea_send.at[0], ea_recv.at[p], p).wait_recv()
+        await_all(sall.at[n, pl.ds(1, N_ROW - 1)], ag_recv.at[n])
+        mine = lax.rem(me, 8) // 2 == n
+        for there, count in ((mine, 3), (jnp.logical_not(mine), 4)):
+
+            @pl.when(there)
+            def _(count=count):
+                await_all(eall.at[pl.ds(0, count)], ea_recv.at[n])
 
         field = sall[n].reshape(width, tile)
         first, last = (jnp.concatenate([eall[p], eall[p + 1]], axis=1) for p in (2 * n, 8 + 2 * n))
@@ -226,8 +234,9 @@
             into[k * width : (k + 1) * width, :] = x
 
     def interpolate(n):
-        def step(r, carry):
-            for k in range(nodes // 256):
+        def step(some, carry):
+            for i in range(4 * (nodes // 256)):
+                r, k = some * 4 + i // (nodes // 256), i % (nodes // 256)
                 at = slice(k * 256, (k + 1) * 256)
                 marks = one_hot(tile, n * tile - 1, low[pl.ds(r, 1), at])
                 both = jnp.dot(vel[...], marks, preferred_element_type=F32)
@@ -236,68 +245,81 @@
                 pvt[r, :, at] = part if n == 0 else pvt[r, :, at] + part
             return carry
 
-        lax.fori_loop(0, levels, step, 0)
-
-    halo_start(0, 2)
+        lax.fori_loop(0, levels // 4, step, 0)
+
+    def slopes(r):
+        center = tv[r + 1]
+        zero = jnp.zeros((1, width), F32)
+        polar = jnp.concatenate([center[1:], zero], axis=0) - jnp.concatenate([zero, center[:-1]], axis=0)
+        slope[r] = sines[...] * (tv[r + 2] - tv[r]) + cosines[...] * polar
+
+    def finish():
+        for side, there, comes in ((0, me > 0, me < N_ROW - 1), (1, me < N_ROW - 1, me > 0)):
+
+            @pl.when(there)
+            def _(side=side):
+                await_all(tv.at[0], h_send.at[side])
+
+            @pl.when(comes)
+            def _(side=side):
+                await_all(tv.at[0], h_recv.at[side])
+
+    plan = iter(zip((0,) + HALO_PLAN, HALO_PLAN))
+    halo_start(*next(plan))
     for n in range(stages):
         sum_columns(n)
         send_inner(n)
         if n > 0:
             send_outer(n - 1)
-        halo_start(n + 2, n + 3)
+        halo_start(*next(plan))
     send_outer(stages - 1)
+    halo_start(*next(plan))
+    for copy in loads[5:]:
+        copy.wait()
+    for r in range(1, levels - 1):
+        slopes(r)
     for n in range(stages):
         reduce_rows(n)
-        halo_start(n + 6, n + 7)
-    halo_start(10, parts)
-    for n in range(stages):
+        halo_start(*next(plan))
+    for n in range(stages - 1):
         velocity(n)
-        if n < stages - 1:
-            interpolate(n)
-    for n in range(stages):
-        for d in range(1, N_ROW):
-            rs_copy(n, d, own.at[n]).wait_send()
-            ag_copy(n, d).wait_send()
-    for d in range(1, N_ROW):
-        e_copy(0, d).wait_send()
-        ea_copy(d).wait_send()
-    for side, there, comes in ((0, me > 0, me < N_ROW - 1), (1, me < N_ROW - 1, me > 0)):
-
-        @pl.when(there)
-        def _(side=side):
-            for k in range(parts):
-                halo(side, k).wait_send()
-
-        @pl.when(comes)
-        def _(side=side):
-            for k in range(parts):
-                halo(side, k).wait_recv()
-
-
-def advance_kernel(tv, pvt, vel, sall, low, off, holder, stream, sines, cosines, out_hbm, flow, out, out_sem):
+        interpolate(n)
+    finish()
+    slopes(0)
+    slopes(levels - 1)
+    velocity(stages - 1)
+    for sem in (rs_send, ag_send):
+        await_all(rs_buf.at[:, pl.ds(1, N_ROW - 1)], sem)
+    for sem in (e_send, ea_send):
+        await_all(rim_buf.at[pl.ds(1, N_ROW - 1)], sem)
+
+
+def advance_kernel(tv, pvt, vel, sall, slope, low, off, holder, stream, out_hbm, flow, drift, out, out_sem):
     levels, nodes, width = out.shape
     cells = holder.shape[1]
     stages, tile = sall.shape[0], sall.shape[3]
     me = lax.axis_index("row")
 
-    def step(r, carry):
+    def interpolate(r):
         for k in range(nodes // 256):
-            lo, hi = k * 256, (k + 1) * 256
-            at = slice(lo, hi)
+            at = slice(k * 256, (k + 1) * 256)
             marks = one_hot(tile, (stages - 1) * tile - 1, low[pl.ds(r, 1), at])
             both = jnp.dot(vel[...], marks, preferred_element_type=F32)
-            drift = pvt[r, :, at] + both[:width] + both[width : 2 * width]
-            drift = drift + off[pl.ds(r, 1), at] * (both[2 * width : 3 * width] + both[3 * width :])
-            drift = drift.T
-            zero = jnp.zeros((1, width), F32)
-            south = jnp.concatenate([tv[r + 1, lo + 1 : hi], zero], axis=0) if hi == nodes else tv[r + 1, lo + 1 : hi + 1]
-            north = jnp.concatenate([zero, tv[r + 1, lo : hi - 1]], axis=0) if lo == 0 else tv[r + 1, lo - 1 : hi - 1]
-            radial = tv[r + 2, at] - tv[r, at]
-            out[r, at] = tv[r + 1, at] - drift * (sines[at] * radial + cosines[at] * (south - north))
+            part = pvt[r, :, at] + both[:width] + both[width : 2 * width]
+            drift[lax.rem(r, 2), :, at] = part + off[pl.ds(r, 1), at] * (both[2 * width : 3 * width] + both[3 * width :])
+
+    def update(r):
+        out[r] = tv[r + 1] - drift[lax.rem(r, 2)].T * slope[r]
         pltpu.make_async_copy(out.at[r], out_hbm.at[r], out_sem.at[r]).start()
+
+    def step(r, carry):
+        update(r - 1)
+        interpolate(r)
         return carry
 
-    lax.fori_loop(0, levels, step, 0)
+    interpolate(0)
+    lax.fori_loop(1, levels, step, 0)
+    update(levels - 1)
     spots = own_slots(holder[...], me, stream.shape[0])
     held = jnp.zeros((2 * width, stream.shape[0]), F32)
     for n in range(stages):
@@ -327,21 +349,22 @@
     params = functools.partial(pltpu.CompilerParams, vmem_limit_bytes=40 << 20)
 
     rows = width // N_ROW
-    parts = 12
     stages = 4
     tile = cells // stages
-    both = lambda: DMA((stages, N_ROW))
-    tv, pvt, vel, sall = pl.pallas_call(
+    tv, pvt, vel, sall, slope = pl.pallas_call(
         fused_kernel,
         out_shape=(
             jax.ShapeDtypeStruct((levels + 2, nodes, width), F32),
             jax.ShapeDtypeStruct((levels, width, nodes), F32),
             jax.ShapeDtypeStruct((4 * width, tile), BF16),
             jax.ShapeDtypeStruct((stages, N_ROW, rows, tile), F32),
+            jax.ShapeDtypeStruct((levels, nodes, width), F32),
         ),
-        in_specs=[HBM] * 6,
-        out_specs=(VMEM,) * 4,
+        in_specs=[HBM] * 8,
+        out_specs=(VMEM,) * 5,
         scratch_shapes=[
+            pltpu.VMEM((nodes, width), F32),
+            pltpu.VMEM((nodes, width), F32),
             pltpu.VMEM((levels, nodes), jnp.int32),
             pltpu.VMEM((levels, nodes), F32),
             pltpu.VMEM((levels, nodes), F32),
@@ -362,24 +385,24 @@
             pltpu.VMEM((width, 128), F32),
             pltpu.VMEM((width, 128), F32),
             pltpu.VMEM((4 * width, tile), BF16),
-            DMA((levels,)), DMA((5,)),
-            both(), both(), both(), both(),
-            DMA((N_ROW,)), DMA((N_ROW,)), DMA((N_ROW,)), DMA((N_ROW,)),
-            DMA((stages, 2)), DMA((stages, 2)), DMA((2, parts)), DMA((2, parts)),
+            DMA((levels,)), DMA((7,)),
+            DMA, DMA((stages,)), DMA, DMA((stages,)),
+            DMA, DMA, DMA, DMA((stages,)),
+            DMA((stages, 2)), DMA((stages, 2)), DMA((2,)), DMA((2,)),
         ],
         compiler_params=params(collective_id=0, has_side_effects=True),
         name="columns",
-    )(*(pltpu.with_memory_space_constraint(x, pltpu.HBM) for x in (heat, lower, offset, share, holder, stream)))
+    )(*(pltpu.with_memory_space_constraint(x, pltpu.HBM) for x in (heat, lower, offset, share, holder, stream, sines, cosines)))
 
     return pl.pallas_call(
         advance_kernel,
         out_shape=(jax.ShapeDtypeStruct(heat.shape, F32), jax.ShapeDtypeStruct((slots, width), F32)),
-        in_specs=[VMEM] * 10,
+        in_specs=[VMEM] * 9,
         out_specs=(HBM, VMEM),
-        scratch_shapes=[pltpu.VMEM((levels, nodes, width), F32), DMA((levels,))],
+        scratch_shapes=[pltpu.VMEM((2, width, nodes), F32), pltpu.VMEM((levels, nodes, width), F32), DMA((levels,))],
         compiler_params=params(),
         name="advance",
-    )(tv, pvt, vel, sall, lower, offset, holder, stream, sines, cosines)
+    )(tv, pvt, vel, sall, slope, lower, offset, holder, stream)
 
 
 def solution(mesh):

time: 56.9 us -> 51.6 us (0.907)
  Pallas kernels: 56.1 us -> 50.6 us
    pallas_call x1, Pallas kernels: 50.3 us -> 45.5 us  [per_device(): pl.pallas_call(fused_kernel, out_shape=(jax.ShapeDtypeStruct((levels + 2,...]
    pallas_call x1, Pallas kernels: 5.8 us -> 5.16 us  [per_device(): pl.pallas_call(advance_kernel, out_shape=(jax.ShapeDtypeStruct(heat.shape...]
where the time goes in v3:
time: 51.6 us; the launch traced here: 51.5 us
  Pallas kernels  50.6 us (98%)
  between operations  0.86 us (2%)
    pallas_call x1, Pallas kernels, per_device(): pl.pallas_call(fused_kernel, out_shape=(jax.ShapeDtypeStruct((levels + 2,...  45.5 us
    pallas_call x1, Pallas kernels, per_device(): pl.pallas_call(advance_kernel, out_shape=(jax.ShapeDtypeStruct(heat.shape...  5.16 us

profile of v3, /device:TPU:2, one launch (start us, length us, event | category | flops | bytes accessed | tf_op | source)
XLA Modules:
  0.0 51.5 jit_solution(8638179972392232005)
XLA Ops:
  0.6 0.0 copy-start
  0.6 0.0 copy-start.2
  0.7 0.0 copy-start.1
  0.7 0.0 copy-start.3
  0.7 45.5 %columns.1 = (f32[10,768,128]{2,1,0:T(8,128)S(1)}, f32[8,128,768]{2,1,0:T(8,128)S(1)}, bf16[512,256]{1,0:T(8,128)(2,1)S(1)}, f32[4,16,8,256]{3,2,1,0:T(8,128)S(1)}, f32[8,768,128]{2,1,0:T(8,128)S(1)}) custom-call(f32[8,768,128]{2,1,0:T(8,128)} %t_hbm.1, s32[8,768]{1,0:T(8,128)} %low.1, f32[8,768]{1,0:T(8,128)} %off.1, f32[8,768]{1,0:T(8,128)} %share_hbm.1, ...), custom_call_target="tpu_custom_call" | custom-call | tf_op jit(solution)/shard_map/columns/pallas_call | solution.py:354
  46.1 0.0 copy-done
  46.2 0.0 copy-done.2
  46.2 0.0 copy-done.1
  46.2 0.0 copy-done.3
  46.2 5.2 %advance.1 = (f32[8,768,128]{2,1,0:T(8,128)}, f32[128,128]{1,0:T(8,128)}) custom-call(f32[10,768,128]{2,1,0:T(8,128)S(1)} %get-tuple-element.7.tv, f32[8,128,768]{2,1,0:T(8,128)S(1)} %get-tuple-element.8.pvt, bf16[512,256]{1,0:T(8,128)(2,1)S(1)} %get-tuple-element.9.vel, f32[4,16,8,256]{3,2,1,0:T(8,128)S(1)} %get-tuple-element.10.sall, ...), custom_call_target="tpu_custom_call" | custom-call | tf_op jit(solution)/shard_map/advance/pallas_call | solution.py:397
Async XLA Ops:
  0.6 45.5 %copy-start = (f32[128,128]{1,0:T(8,128)S(1)}, f32[128,128]{1,0:T(8,128)}, u32[]{:S(2)}) copy-start(f32[128,128]{1,0:T(8,128)} %stream.1) | copy-start | bytes 196612
  0.6 45.5 %copy-start.2 = (f32[8,768]{1,0:T(8,128)S(1)}, f32[8,768]{1,0:T(8,128)}, u32[]{:S(2)}) copy-start(f32[8,768]{1,0:T(8,128)} %off.1) | copy-start | bytes 73732
  0.7 45.5 %copy-start.1 = (s32[8,768]{1,0:T(8,128)S(1)}, s32[8,768]{1,0:T(8,128)}, u32[]{:S(2)}) copy-start(s32[8,768]{1,0:T(8,128)} %low.1) | copy-start | bytes 73732
  0.7 45.5 %copy-start.3 = (s32[1024]{0:T(1024)S(1)}, s32[1024]{0:T(1024)}, u32[]{:S(2)}) copy-start(s32[1024]{0:T(1024)} %param.12) | copy-start | bytes 12292

commit v4 on v3

--- a/solution.py
+++ b/solution.py
@@ -13,8 +13,10 @@
 F32 = jnp.float32
 BF16 = jnp.bfloat16
 N_ROW = 16
+N_PAIR = 8
 N_MA = 16
-HALO_PLAN = (2, 3, 4, 5, 6, 7, 8, 9, 10, 12)
+HALO_PLAN = (2, 3, 4, 4, 5, 7, 8, 9, 10, 12)
+Y_LAST = (0, 1, 2, 3)
 NT = (((1,), (1,)), ((), ()))
 
 
@@ -31,6 +33,11 @@
 def geo_row(cells, first, count):
     c = (first + lax.broadcasted_iota(jnp.int32, (1, count), 1)).astype(F32)
     return 1.0 / (0.25 + (c + 0.5) / cells)
+
+
+def by_azimuth(gathered, n):
+    half, pairs, rows, tile = gathered.shape[1:]
+    return jnp.stack([gathered[n, k] for k in range(half)], axis=1).reshape(half * pairs * rows, tile)
 
 
 def own_slots(holder, me, slots):
@@ -43,13 +50,15 @@
 def fused_kernel(
     t_hbm, low_hbm, off_hbm, share_hbm, holder_hbm, stream_hbm, sin_hbm, cos_hbm,
     tv, pvt, vel_last, sall, slope,
-    sines, cosines, low, off, share, holder, stream_in, stream, twt, sp, edge, rim, ends, rim_send, rs_buf, rim_buf, own, rim_own, eall, carry_up, carry_vel, vel,
-    t_sem, in_sem, rs_send, rs_recv, ag_send, ag_recv, e_send, e_recv, ea_send, ea_recv, ma_send, ma_recv, h_send, h_recv,
+    sines, cosines, low, off, share, holder, stream_in, stream, twt, sp, pair_in, pair, edge, rim, fix, fix_in, rim_send, rs_buf, rim_buf, own, rim_own, eall, carry_up, carry_vel, vel,
+    t_sem, in_sem, y_send, y_recv, fix_send, fix_recv, rs_send, rs_recv, ag_send, ag_recv, agy_send, agy_recv, e_send, e_recv, ea_send, ea_recv, ma_send, ma_recv, h_send, h_recv,
 ):
     levels, width, nodes = pvt.shape
     cells = holder.shape[1]
-    stages, tile = sp.shape[0], sp.shape[3]
+    stages, tile = sp.shape[0], sp.shape[4]
     me = lax.axis_index("row")
+    side_y, at_z = lax.rem(me, 2), me // 2
+    partner = me + 1 - 2 * side_y
     ma = lax.axis_index("ma")
     right, left = lax.rem(ma + 1, N_MA), lax.rem(ma + N_MA - 1, N_MA)
     parts = HALO_PLAN[-1]
@@ -79,8 +88,8 @@
     spots = own_slots(holder[...], me, stream_in.shape[0])
     placed = jnp.dot(jnp.concatenate(two_parts(stream_in[...].T), axis=0), spots, preferred_element_type=F32)
     stream[...] = placed[:width] + placed[width:]
-    for r in range(levels):
-        heat_loads[r].wait()
+
+    def prepare(r):
         weights = share[r : r + 1, :]
         offset = off[r : r + 1, :]
         heat = tv[r + 1].T
@@ -89,7 +98,6 @@
             twt[r, 2 * k * width : (2 * k + 1) * width, :] = hi
             twt[r, (2 * k + 1) * width : (2 * k + 2) * width, :] = lo
 
-    pl.semaphore_wait(barrier, N_ROW + 1)
 
     def to_row(src, dst, send, recv, peer):
         return pltpu.make_async_remote_copy(src_ref=src, dst_ref=dst, send_sem=send, recv_sem=recv, device_id={"row": peer}, device_id_type=MESH)
@@ -120,11 +128,42 @@
             for k, side in enumerate((left, right))
         ]
 
-    def rs_copy(n, d, src):
-        return to_row(src, rs_buf.at[n, d], rs_send, rs_recv.at[n], lax.rem(me + d, N_ROW))
-
-    def ag_copy(n, d):
-        return to_row(own.at[n], sall.at[n, me], ag_send, ag_recv.at[n], lax.rem(me + d, N_ROW))
+    def y_copy(n):
+        return to_row(sp.at[n, 1 - side_y], pair_in.at[n], y_send, y_recv.at[n], partner)
+
+    def rs_copy(n, dz):
+        z = lax.rem(at_z + dz, N_PAIR)
+        return to_row(pair.at[n, z], rs_buf.at[n, dz], rs_send, rs_recv.at[n], 2 * z + side_y)
+
+    def fix_copy(n, k, p):
+        d = lax.rem(p - me + N_ROW, N_ROW)
+        return to_row(fix.at[n, k], fix_in.at[n, d], fix_send, fix_recv.at[n], p)
+
+    def gather_first(n):
+        if n in Y_LAST:
+            peers = [2 * lax.rem(at_z + dz, N_PAIR) + side_y for dz in range(1, N_PAIR)]
+        else:
+            peers = [lax.rem(me + d, N_ROW) for d in range(1, N_ROW)]
+        for peer in peers:
+            to_row(own.at[n], sall.at[n, side_y, at_z], ag_send.at[n], ag_recv.at[n], peer).start()
+
+    def forward(n):
+        if n in Y_LAST:
+            await_all(rs_buf.at[n, pl.ds(1, N_PAIR - 1)], ag_recv.at[n])
+            to_row(sall.at[n, side_y], sall.at[n, side_y], agy_send.at[n], agy_recv.at[n], partner).start()
+
+    def await_gathered(n):
+        if n in Y_LAST:
+            await_all(pair.at[n], agy_recv.at[n])
+        else:
+            await_all(rs_buf.at[pl.ds(0, 3), pl.ds(0, 5)], ag_recv.at[n])
+
+    def await_sent(n):
+        if n in Y_LAST:
+            await_all(rs_buf.at[n, pl.ds(1, N_PAIR - 1)], ag_send.at[n])
+            await_all(pair.at[n], agy_send.at[n])
+        else:
+            await_all(rs_buf.at[pl.ds(0, 3), pl.ds(0, 5)], ag_send.at[n])
 
     def e_copy(p, d):
         return to_row(rim_send.at[p], rim_buf.at[d], e_send, e_recv, p)
@@ -135,6 +174,14 @@
     def sum_columns(n):
         sums = [jnp.zeros((4 * width, tile), F32)] * 2
         for r in range(levels):
+            if n == 0:
+                if r % 4 == 0:
+                    for copy in heat_loads[r : r + 4]:
+                        copy.wait()
+                if r == 4:
+                    pl.semaphore_wait(barrier, N_ROW + 1)
+                    halo_start(*next(plan))
+                prepare(r)
             marks = one_hot(tile, n * tile, low[r : r + 1, :])
             sums[r % 2] = sums[r % 2] + lax.dot_general(twt[r], marks, NT, preferred_element_type=F32)
         half = 2 * width
@@ -152,28 +199,22 @@
         ahead = jnp.concatenate([zint[1:], zero], axis=0)
         behind = jnp.concatenate([zero, zint[:-1]], axis=0)
         partial = stream[:, n * tile : (n + 1) * tile] - (ahead - behind)
-        sp[n] = partial.reshape(N_ROW, width // N_ROW, tile)
+        chunks = partial.reshape(N_PAIR, 2, width // N_ROW, tile)
+        for k in range(2):
+            sp[n, k] = chunks[:, k]
         edge[n, 0] = jnp.concatenate([zint[:1], partial[:1]], axis=0)
         edge[n, 1] = jnp.concatenate([zint[-1:], partial[-1:]], axis=0)
 
     def send_inner(n):
         for copy in rim_copies(n):
             copy.start()
-        for d in range(1, N_ROW):
-            peer = lax.rem(me + d, N_ROW)
-
-            @pl.when(jnp.logical_and(peer > 0, peer < N_ROW - 1))
-            def _(d=d, peer=peer):
-                rs_copy(n, d, sp.at[n, peer]).start()
+        y_copy(n).start()
 
     def send_outer(n):
         for copy in rim_copies(n):
             copy.wait()
-        last = width // N_ROW - 1
-        ends[n, 0] = sp[n, 0]
-        ends[n, 1] = sp[n, N_ROW - 1]
-        ends[n, 0, 0:1] = sp[n, 0, 0:1] + rim[n, 1, 0:1]
-        ends[n, 1, last : last + 1] = sp[n, N_ROW - 1, last : last + 1] - rim[n, 0, 0:1]
+        fix[n, 0] = rim[n, 1, 0:1]
+        fix[n, 1] = rim[n, 0, 0:1]
         outer = (rim[n, 1, 1:2] - edge[n, 0, 0:1], rim[n, 0, 1:2] + edge[n, 1, 0:1])
         for i, p in enumerate(pieces(n)):
             rim_send[p] = outer[i // 2][:, (i % 2) * 128 : (i % 2 + 1) * 128]
@@ -181,7 +222,7 @@
 
             @pl.when(me != p)
             def _(k=k, p=p):
-                rs_copy(n, lax.rem(p - me + N_ROW, N_ROW), ends.at[n, k]).start()
+                fix_copy(n, k, p).start()
 
         for p in pieces(n):
 
@@ -189,15 +230,30 @@
             def _(p=p):
                 e_copy(p, lax.rem(p - me + N_ROW, N_ROW)).start()
 
+    def pair_rows(n):
+        await_all(pair_in.at[n], y_recv.at[n])
+        pair[n] = sp[n, side_y] + pair_in[n]
+        for dz in range(1, N_PAIR):
+            rs_copy(n, dz).start()
+
     def reduce_rows(n):
-        total = jnp.where(me == 0, ends[n, 0], jnp.where(me == N_ROW - 1, ends[n, 1], sp[n, me]))
-        await_all(rs_buf.at[n, pl.ds(1, N_ROW - 1)], rs_recv.at[n])
-        for d in range(1, N_ROW):
-            total = total + rs_buf[n, d]
+        await_all(rs_buf.at[n, pl.ds(1, N_PAIR - 1)], rs_recv.at[n])
+        total = pair[n, at_z]
+        for dz in range(1, N_PAIR):
+            total = total + rs_buf[n, dz]
         own[n] = total
-        sall[n, me] = total
-        for d in range(1, N_ROW):
-            ag_copy(n, d).start()
+        for k, (p, at, sign) in enumerate(((0, 0, 1.0), (N_ROW - 1, width // N_ROW - 1, -1.0))):
+
+            @pl.when(me == p)
+            def _(k=k, at=at, sign=sign):
+                await_all(fix_in.at[n, pl.ds(1, N_ROW - 1)], fix_recv.at[n])
+                more = fix[n, k]
+                for d in range(1, N_ROW):
+                    more = more + fix_in[n, d]
+                own[n, at : at + 1] = own[n, at : at + 1] + sign * more
+
+        sall[n, side_y, at_z] = own[n]
+        gather_first(n)
 
         @pl.when(lax.rem(me, 8) // 2 == n)
         def _():
@@ -211,7 +267,7 @@
                 ea_copy(d).start()
 
     def velocity(n):
-        await_all(sall.at[n, pl.ds(1, N_ROW - 1)], ag_recv.at[n])
+        await_gathered(n)
         mine = lax.rem(me, 8) // 2 == n
         for there, count in ((mine, 3), (jnp.logical_not(mine), 4)):
 
@@ -219,7 +275,7 @@
             def _(count=count):
                 await_all(eall.at[pl.ds(0, count)], ea_recv.at[n])
 
-        field = sall[n].reshape(width, tile)
+        field = by_azimuth(sall, n)
         first, last = (jnp.concatenate([eall[p], eall[p + 1]], axis=1) for p in (2 * n, 8 + 2 * n))
         ahead = jnp.concatenate([field[1:], last], axis=0)
         behind = jnp.concatenate([first, field[:-1]], axis=0)
@@ -265,31 +321,55 @@
                 await_all(tv.at[0], h_recv.at[side])
 
     plan = iter(zip((0,) + HALO_PLAN, HALO_PLAN))
-    halo_start(*next(plan))
     for n in range(stages):
         sum_columns(n)
         send_inner(n)
         if n > 0:
             send_outer(n - 1)
+        if n > 1:
+            pair_rows(n - 2)
         halo_start(*next(plan))
-    send_outer(stages - 1)
-    halo_start(*next(plan))
     for copy in loads[5:]:
         copy.wait()
     for r in range(1, levels - 1):
         slopes(r)
-    for n in range(stages):
-        reduce_rows(n)
-        halo_start(*next(plan))
-    for n in range(stages - 1):
-        velocity(n)
-        interpolate(n)
+    pair_rows(2)
+    reduce_rows(0)
+    send_outer(3)
+    halo_start(*next(plan))
+    pair_rows(3)
+    halo_start(*next(plan))
+    reduce_rows(1)
+    halo_start(*next(plan))
+    forward(0)
+    reduce_rows(2)
+    halo_start(*next(plan))
+    reduce_rows(3)
+    forward(1)
+    halo_start(*next(plan))
+    velocity(0)
+    interpolate(0)
+    forward(2)
+    velocity(1)
+    forward(3)
+    interpolate(1)
+    velocity(2)
+    interpolate(2)
     finish()
     slopes(0)
     slopes(levels - 1)
     velocity(stages - 1)
-    for sem in (rs_send, ag_send):
-        await_all(rs_buf.at[:, pl.ds(1, N_ROW - 1)], sem)
+    await_all(pair_in, y_send)
+    await_all(rs_buf.at[:, pl.ds(1, N_PAIR - 1)], rs_send)
+    for n in range(stages):
+        await_sent(n)
+    inner = jnp.logical_and(me > 0, me < N_ROW - 1)
+    for there, count in ((inner, 8), (jnp.logical_not(inner), 4)):
+
+        @pl.when(there)
+        def _(count=count):
+            await_all(fix_in.at[0, pl.ds(0, count)], fix_send)
+
     for sem in (e_send, ea_send):
         await_all(rim_buf.at[pl.ds(1, N_ROW - 1)], sem)
 
@@ -297,10 +377,10 @@
 def advance_kernel(tv, pvt, vel, sall, slope, low, off, holder, stream, out_hbm, flow, drift, out, out_sem):
     levels, nodes, width = out.shape
     cells = holder.shape[1]
-    stages, tile = sall.shape[0], sall.shape[3]
+    stages, tile = sall.shape[0], sall.shape[4]
     me = lax.axis_index("row")
 
-    def interpolate(r):
+    def blend(r):
         for k in range(nodes // 256):
             at = slice(k * 256, (k + 1) * 256)
             marks = one_hot(tile, (stages - 1) * tile - 1, low[pl.ds(r, 1), at])
@@ -314,16 +394,16 @@
 
     def step(r, carry):
         update(r - 1)
-        interpolate(r)
+        blend(r)
         return carry
 
-    interpolate(0)
-    lax.fori_loop(1, levels, step, 0)
+    blend(0)
+    lax.fori_loop(1, levels, step, 0, unroll=levels - 1)
     update(levels - 1)
     spots = own_slots(holder[...], me, stream.shape[0])
     held = jnp.zeros((2 * width, stream.shape[0]), F32)
     for n in range(stages):
-        field = jnp.concatenate(two_parts(sall[n].reshape(width, tile)), axis=0)
+        field = jnp.concatenate(two_parts(by_azimuth(sall, n)), axis=0)
         held = held + lax.dot_general(field, spots[:, n * tile : (n + 1) * tile], NT, preferred_element_type=F32)
     held = (held[:width] + held[width:]).T
     count = jnp.sum((holder[...] == me).astype(F32), axis=1, keepdims=True).astype(jnp.int32)
@@ -357,7 +437,7 @@
             jax.ShapeDtypeStruct((levels + 2, nodes, width), F32),
             jax.ShapeDtypeStruct((levels, width, nodes), F32),
             jax.ShapeDtypeStruct((4 * width, tile), BF16),
-            jax.ShapeDtypeStruct((stages, N_ROW, rows, tile), F32),
+            jax.ShapeDtypeStruct((stages, 2, N_PAIR, rows, tile), F32),
             jax.ShapeDtypeStruct((levels, nodes, width), F32),
         ),
         in_specs=[HBM] * 8,
@@ -372,12 +452,15 @@
             pltpu.VMEM((slots, width), F32),
             pltpu.VMEM((width, cells), F32),
             pltpu.VMEM((levels, 4 * width, nodes), BF16),
-            pltpu.VMEM((stages, N_ROW, rows, tile), F32),
+            pltpu.VMEM((stages, 2, N_PAIR, rows, tile), F32),
+            pltpu.VMEM((stages, N_PAIR, rows, tile), F32),
+            pltpu.VMEM((stages, N_PAIR, rows, tile), F32),
             pltpu.VMEM((stages, 2, 2, tile), F32),
             pltpu.VMEM((stages, 2, 2, tile), F32),
-            pltpu.VMEM((stages, 2, rows, tile), F32),
+            pltpu.VMEM((stages, 2, 1, tile), F32),
+            pltpu.VMEM((stages, N_ROW, 1, tile), F32),
             pltpu.VMEM((N_ROW, 1, 128), F32),
-            pltpu.VMEM((stages, N_ROW, rows, tile), F32),
+            pltpu.VMEM((stages, N_PAIR, rows, tile), F32),
             pltpu.VMEM((N_ROW, 1, 128), F32),
             pltpu.VMEM((stages, rows, tile), F32),
             pltpu.VMEM((1, 128), F32),
@@ -387,6 +470,7 @@
             pltpu.VMEM((4 * width, tile), BF16),
             DMA((levels,)), DMA((7,)),
             DMA, DMA((stages,)), DMA, DMA((stages,)),
+            DMA, DMA((stages,)), DMA((stages,)), DMA((stages,)), DMA((stages,)), DMA((stages,)),
             DMA, DMA, DMA, DMA((stages,)),
             DMA((stages, 2)), DMA((stages, 2)), DMA((2,)), DMA((2,)),
         ],

time: 51.6 us -> 48.9 us (0.948)
  Pallas kernels: 50.6 us -> 48 us
    pallas_call x1, Pallas kernels: 45.5 us -> 43.9 us  [per_device(): pl.pallas_call(fused_kernel, out_shape=(jax.ShapeDtypeStruct((levels + 2,...]
    pallas_call x1, Pallas kernels: 5.16 us -> 4.06 us  [per_device(): pl.pallas_call(advance_kernel, out_shape=(jax.ShapeDtypeStruct(heat.shape...]
where the time goes in v4:
time: 48.9 us; the launch traced here: 48.8 us
  Pallas kernels  48 us (98%)
  between operations  0.86 us (2%)
    pallas_call x1, Pallas kernels, per_device(): pl.pallas_call(fused_kernel, out_shape=(jax.ShapeDtypeStruct((levels + 2,...  43.9 us
    pallas_call x1, Pallas kernels, per_device(): pl.pallas_call(advance_kernel, out_shape=(jax.ShapeDtypeStruct(heat.shape...  4.06 us

profile of v4, /device:TPU:2, one launch (start us, length us, event | category | flops | bytes accessed | tf_op | source)
XLA Modules:
  0.0 48.8 jit_solution(12219579578517602374)
XLA Ops:
  0.6 0.0 copy-start
  0.6 0.0 copy-start.2
  0.7 0.0 copy-start.1
  0.7 0.0 copy-start.3
  0.7 43.9 %columns.1 = (f32[10,768,128]{2,1,0:T(8,128)S(1)}, f32[8,128,768]{2,1,0:T(8,128)S(1)}, bf16[512,256]{1,0:T(8,128)(2,1)S(1)}, f32[4,2,8,8,256]{4,3,2,1,0:T(8,128)S(1)}, f32[8,768,128]{2,1,0:T(8,128)S(1)}) custom-call(f32[8,768,128]{2,1,0:T(8,128)} %t_hbm.1, s32[8,768]{1,0:T(8,128)} %low.1, f32[8,768]{1,0:T(8,128)} %off.1, f32[8,768]{1,0:T(8,128)} %share_hbm.1, ...), custom_call_target="tpu_custom_call" | custom-call | tf_op jit(solution)/shard_map/columns/pallas_call | solution.py:434
  44.6 0.0 copy-done
  44.6 0.0 copy-done.2
  44.6 0.0 copy-done.1
  44.6 0.0 copy-done.3
  44.6 4.1 %advance.1 = (f32[8,768,128]{2,1,0:T(8,128)}, f32[128,128]{1,0:T(8,128)}) custom-call(f32[10,768,128]{2,1,0:T(8,128)S(1)} %get-tuple-element.7.tv, f32[8,128,768]{2,1,0:T(8,128)S(1)} %get-tuple-element.8.pvt, bf16[512,256]{1,0:T(8,128)(2,1)S(1)} %get-tuple-element.9.vel, f32[4,2,8,8,256]{4,3,2,1,0:T(8,128)S(1)} %get-tuple-element.10.sall, ...), custom_call_target="tpu_custom_call" | custom-call | tf_op jit(solution)/shard_map/advance/pallas_call | solution.py:481
Async XLA Ops:
  0.6 43.9 %copy-start = (f32[128,128]{1,0:T(8,128)S(1)}, f32[128,128]{1,0:T(8,128)}, u32[]{:S(2)}) copy-start(f32[128,128]{1,0:T(8,128)} %stream.1) | copy-start | bytes 196612
  0.6 43.9 %copy-start.2 = (f32[8,768]{1,0:T(8,128)S(1)}, f32[8,768]{1,0:T(8,128)}, u32[]{:S(2)}) copy-start(f32[8,768]{1,0:T(8,128)} %off.1) | copy-start | bytes 73732
  0.7 43.9 %copy-start.1 = (s32[8,768]{1,0:T(8,128)S(1)}, s32[8,768]{1,0:T(8,128)}, u32[]{:S(2)}) copy-start(s32[8,768]{1,0:T(8,128)} %low.1) | copy-start | bytes 73732
  0.7 43.9 %copy-start.3 = (s32[1024]{0:T(1024)S(1)}, s32[1024]{0:T(1024)}, u32[]{:S(2)}) copy-start(s32[1024]{0:T(1024)} %param.12) | copy-start | bytes 12292

commit v5 on v4

--- a/solution.py
+++ b/solution.py
@@ -15,8 +15,8 @@
 N_ROW = 16
 N_PAIR = 8
 N_MA = 16
-HALO_PLAN = (2, 3, 4, 4, 5, 7, 8, 9, 10, 12)
-Y_LAST = (0, 1, 2, 3)
+HALO_PLAN = (2, 3, 3, 3, 5, 6, 7, 8, 9, 12)
+Y_LAST = (0, 1)
 NT = (((1,), (1,)), ((), ()))
 
 
@@ -139,31 +139,37 @@
         d = lax.rem(p - me + N_ROW, N_ROW)
         return to_row(fix.at[n, k], fix_in.at[n, d], fix_send, fix_recv.at[n], p)
 
+    def along_z(src, n, half):
+        for dz in range(1, N_PAIR):
+            peer = 2 * lax.rem(at_z + dz, N_PAIR) + side_y
+            to_row(src, sall.at[n, half, at_z], ag_send.at[n], ag_recv.at[n], peer).start()
+
     def gather_first(n):
-        if n in Y_LAST:
-            peers = [2 * lax.rem(at_z + dz, N_PAIR) + side_y for dz in range(1, N_PAIR)]
-        else:
-            peers = [lax.rem(me + d, N_ROW) for d in range(1, N_ROW)]
-        for peer in peers:
-            to_row(own.at[n], sall.at[n, side_y, at_z], ag_send.at[n], ag_recv.at[n], peer).start()
+        if n not in Y_LAST:
+            to_row(own.at[n], sall.at[n, side_y, at_z], agy_send.at[n], agy_recv.at[n], partner).start()
+        along_z(own.at[n], n, side_y)
 
     def forward(n):
         if n in Y_LAST:
             await_all(rs_buf.at[n, pl.ds(1, N_PAIR - 1)], ag_recv.at[n])
             to_row(sall.at[n, side_y], sall.at[n, side_y], agy_send.at[n], agy_recv.at[n], partner).start()
+        else:
+            await_all(own.at[n], agy_recv.at[n])
+            along_z(sall.at[n, 1 - side_y, at_z], n, 1 - side_y)
 
     def await_gathered(n):
         if n in Y_LAST:
             await_all(pair.at[n], agy_recv.at[n])
         else:
-            await_all(rs_buf.at[pl.ds(0, 3), pl.ds(0, 5)], ag_recv.at[n])
+            await_all(rs_buf.at[pl.ds(0, 2), pl.ds(1, N_PAIR - 1)], ag_recv.at[n])
 
     def await_sent(n):
         if n in Y_LAST:
             await_all(rs_buf.at[n, pl.ds(1, N_PAIR - 1)], ag_send.at[n])
             await_all(pair.at[n], agy_send.at[n])
         else:
-            await_all(rs_buf.at[pl.ds(0, 3), pl.ds(0, 5)], ag_send.at[n])
+            await_all(rs_buf.at[pl.ds(0, 2), pl.ds(1, N_PAIR - 1)], ag_send.at[n])
+            await_all(own.at[n], agy_send.at[n])
 
     def e_copy(p, d):
         return to_row(rim_send.at[p], rim_buf.at[d], e_send, e_recv, p)
@@ -301,7 +307,7 @@
                 pvt[r, :, at] = part if n == 0 else pvt[r, :, at] + part
             return carry
 
-        lax.fori_loop(0, levels // 4, step, 0)
+        lax.fori_loop(0, levels // 4, step, 0, unroll=2)
 
     def slopes(r):
         center = tv[r + 1]
@@ -345,13 +351,13 @@
     reduce_rows(2)
     halo_start(*next(plan))
     reduce_rows(3)
+    forward(2)
     forward(1)
     halo_start(*next(plan))
     velocity(0)
+    forward(3)
     interpolate(0)
-    forward(2)
     velocity(1)
-    forward(3)
     interpolate(1)
     velocity(2)
     interpolate(2)

time: 48.9 us -> 48.2 us (0.986); the launches traced: 48.8 us -> 47.6 us
  Pallas kernels: 48 us -> 46.7 us
    pallas_call x1, Pallas kernels: 43.9 us -> 42.6 us  [per_device(): pl.pallas_call(fused_kernel, out_shape=(jax.ShapeDtypeStruct((levels + 2,...]
where the time goes in v5:
time: 48.2 us; the launch traced here: 47.6 us
  Pallas kernels  46.7 us (97%)
  between operations  0.86 us (2%)
    pallas_call x1, Pallas kernels, per_device(): pl.pallas_call(fused_kernel, out_shape=(jax.ShapeDtypeStruct((levels + 2,...  42.6 us
    pallas_call x1, Pallas kernels, per_device(): pl.pallas_call(advance_kernel, out_shape=(jax.ShapeDtypeStruct(heat.shape...  4.07 us

profile of v5, /device:TPU:2, one launch (start us, length us, event | category | flops | bytes accessed | tf_op | source)
XLA Modules:
  0.0 47.6 jit_solution(7740030870670787637)
XLA Ops:
  0.6 0.0 copy-start
  0.6 0.0 copy-start.2
  0.7 0.0 copy-start.1
  0.7 0.0 copy-start.3
  0.7 42.6 %columns.1 = (f32[10,768,128]{2,1,0:T(8,128)S(1)}, f32[8,128,768]{2,1,0:T(8,128)S(1)}, bf16[512,256]{1,0:T(8,128)(2,1)S(1)}, f32[4,2,8,8,256]{4,3,2,1,0:T(8,128)S(1)}, f32[8,768,128]{2,1,0:T(8,128)S(1)}) custom-call(f32[8,768,128]{2,1,0:T(8,128)} %t_hbm.1, s32[8,768]{1,0:T(8,128)} %low.1, f32[8,768]{1,0:T(8,128)} %off.1, f32[8,768]{1,0:T(8,128)} %share_hbm.1, ...), custom_call_target="tpu_custom_call" | custom-call | tf_op jit(solution)/shard_map/columns/pallas_call | solution.py:440
  43.3 0.0 copy-done
  43.3 0.0 copy-done.2
  43.3 0.0 copy-done.1
  43.3 0.0 copy-done.3
  43.3 4.1 %advance.1 = (f32[8,768,128]{2,1,0:T(8,128)}, f32[128,128]{1,0:T(8,128)}) custom-call(f32[10,768,128]{2,1,0:T(8,128)S(1)} %get-tuple-element.7.tv, f32[8,128,768]{2,1,0:T(8,128)S(1)} %get-tuple-element.8.pvt, bf16[512,256]{1,0:T(8,128)(2,1)S(1)} %get-tuple-element.9.vel, f32[4,2,8,8,256]{4,3,2,1,0:T(8,128)S(1)} %get-tuple-element.10.sall, ...), custom_call_target="tpu_custom_call" | custom-call | tf_op jit(solution)/shard_map/advance/pallas_call | solution.py:487
Async XLA Ops:
  0.6 42.7 %copy-start = (f32[128,128]{1,0:T(8,128)S(1)}, f32[128,128]{1,0:T(8,128)}, u32[]{:S(2)}) copy-start(f32[128,128]{1,0:T(8,128)} %stream.1) | copy-start | bytes 196612
  0.6 42.7 %copy-start.2 = (f32[8,768]{1,0:T(8,128)S(1)}, f32[8,768]{1,0:T(8,128)}, u32[]{:S(2)}) copy-start(f32[8,768]{1,0:T(8,128)} %off.1) | copy-start | bytes 73732
  0.7 42.7 %copy-start.1 = (s32[8,768]{1,0:T(8,128)S(1)}, s32[8,768]{1,0:T(8,128)}, u32[]{:S(2)}) copy-start(s32[8,768]{1,0:T(8,128)} %low.1) | copy-start | bytes 73732
  0.7 42.7 %copy-start.3 = (s32[1024]{0:T(1024)S(1)}, s32[1024]{0:T(1024)}, u32[]{:S(2)}) copy-start(s32[1024]{0:T(1024)} %param.12) | copy-start | bytes 12292

commit v6 on v5

--- a/solution.py
+++ b/solution.py
@@ -16,7 +16,7 @@
 N_PAIR = 8
 N_MA = 16
 HALO_PLAN = (2, 3, 3, 3, 5, 6, 7, 8, 9, 12)
-Y_LAST = (0, 1)
+Y_LAST = (0,)
 NT = (((1,), (1,)), ((), ()))
 
 
@@ -347,12 +347,12 @@
     halo_start(*next(plan))
     reduce_rows(1)
     halo_start(*next(plan))
+    forward(1)
     forward(0)
     reduce_rows(2)
     halo_start(*next(plan))
     reduce_rows(3)
     forward(2)
-    forward(1)
     halo_start(*next(plan))
     velocity(0)
     forward(3)

time: 48.2 us -> 48.3 us (level); the launches traced: 47.6 us -> 48.2 us
  Pallas kernels: 46.7 us -> 47.3 us
    pallas_call x1, Pallas kernels: 42.6 us -> 43.2 us  [per_device(): pl.pallas_call(fused_kernel, out_shape=(jax.ShapeDtypeStruct((levels + 2,...]
where the time goes in v6:
time: 48.3 us; the launch traced here: 48.2 us
  Pallas kernels  47.3 us (98%)
  between operations  0.86 us (2%)
    pallas_call x1, Pallas kernels, per_device(): pl.pallas_call(fused_kernel, out_shape=(jax.ShapeDtypeStruct((levels + 2,...  43.2 us
    pallas_call x1, Pallas kernels, per_device(): pl.pallas_call(advance_kernel, out_shape=(jax.ShapeDtypeStruct(heat.shape...  4.06 us

profile of v6, /device:TPU:2, one launch (start us, length us, event | category | flops | bytes accessed | tf_op | source)
XLA Modules:
  0.0 48.2 jit_solution(15239040596442704286)
XLA Ops:
  0.6 0.0 copy-start
  0.6 0.0 copy-start.2
  0.7 0.0 copy-start.1
  0.7 0.0 copy-start.3
  0.7 43.2 %columns.1 = (f32[10,768,128]{2,1,0:T(8,128)S(1)}, f32[8,128,768]{2,1,0:T(8,128)S(1)}, bf16[512,256]{1,0:T(8,128)(2,1)S(1)}, f32[4,2,8,8,256]{4,3,2,1,0:T(8,128)S(1)}, f32[8,768,128]{2,1,0:T(8,128)S(1)}) custom-call(f32[8,768,128]{2,1,0:T(8,128)} %t_hbm.1, s32[8,768]{1,0:T(8,128)} %low.1, f32[8,768]{1,0:T(8,128)} %off.1, f32[8,768]{1,0:T(8,128)} %share_hbm.1, ...), custom_call_target="tpu_custom_call" | custom-call | tf_op jit(solution)/shard_map/columns/pallas_call | solution.py:440
  43.9 0.0 copy-done
  43.9 0.0 copy-done.2
  43.9 0.0 copy-done.1
  43.9 0.0 copy-done.3
  44.0 4.1 %advance.1 = (f32[8,768,128]{2,1,0:T(8,128)}, f32[128,128]{1,0:T(8,128)}) custom-call(f32[10,768,128]{2,1,0:T(8,128)S(1)} %get-tuple-element.7.tv, f32[8,128,768]{2,1,0:T(8,128)S(1)} %get-tuple-element.8.pvt, bf16[512,256]{1,0:T(8,128)(2,1)S(1)} %get-tuple-element.9.vel, f32[4,2,8,8,256]{4,3,2,1,0:T(8,128)S(1)} %get-tuple-element.10.sall, ...), custom_call_target="tpu_custom_call" | custom-call | tf_op jit(solution)/shard_map/advance/pallas_call | solution.py:487
Async XLA Ops:
  0.6 43.3 %copy-start = (f32[128,128]{1,0:T(8,128)S(1)}, f32[128,128]{1,0:T(8,128)}, u32[]{:S(2)}) copy-start(f32[128,128]{1,0:T(8,128)} %stream.1) | copy-start | bytes 196612
  0.6 43.3 %copy-start.2 = (f32[8,768]{1,0:T(8,128)S(1)}, f32[8,768]{1,0:T(8,128)}, u32[]{:S(2)}) copy-start(f32[8,768]{1,0:T(8,128)} %off.1) | copy-start | bytes 73732
  0.7 43.3 %copy-start.1 = (s32[8,768]{1,0:T(8,128)S(1)}, s32[8,768]{1,0:T(8,128)}, u32[]{:S(2)}) copy-start(s32[8,768]{1,0:T(8,128)} %low.1) | copy-start | bytes 73732
  0.7 43.3 %copy-start.3 = (s32[1024]{0:T(1024)S(1)}, s32[1024]{0:T(1024)}, u32[]{:S(2)}) copy-start(s32[1024]{0:T(1024)} %param.12) | copy-start | bytes 12292
